TPU v7x, 32 devices: a whole 2x2x4 slice. The times are simulated.
32 devices in a mesh: pts: 8 (over y, x, core), wid: 4 (over z).
Axes of the slice: x: 2, y: 2, z: 4, core: 2. Of those that a mesh axis runs over, the one named last changes fastest.
Arguments:
- vertex_features: bfloat16 [90112, 512], P('pts'), may hold values from -40 to 40, as said below
- entry_matrix: bfloat16 [512, 512], P(None, 'wid'), may hold values from -2 to 2, as said below
- partition_matrix: bfloat16 [64, 32], replicated, may hold values from -3 to 3, as said below
- sharpness_matrix: float32 [64], replicated, may hold values from -3 to 3, as said below
- summary_qkv_matrix: float32 [3, 64, 64], replicated, may hold values from -3 to 3
- exit_matrix: bfloat16 [512, 512], P('wid'), may hold values from -0.5 to 0.5
- widening_matrix: bfloat16 [512, 512], P('wid'), may hold values from -0.25 to 0.25
- narrowing_matrix: bfloat16 [512, 512], P('wid'), may hold values from -0.25 to 0.25
Outputs:
- result: bfloat16 [90112, 512], P(('pts', 'wid'))
Inputs may be any that keep to these rules, and one draw needn't show every extreme that they name: `vertex_features`: features of the points, of order one to ten. `entry_matrix`: weights of the point projection. `partition_matrix`: slice logit weights. `sharpness_matrix`: temperature weights.
All inputs are finite; a program needn't handle non-finite values.
Results may differ from a plain program's by a relative error of at most 0.013.
Values may be sent and summed in bfloat16 or wider, within the bound.
A program may use at most 128 MiB of HBM per device.

v0:
```python
import functools

import jax
import jax.numpy as jnp
from jax import lax
from jax.experimental import pallas as pl
from jax.experimental.pallas import tpu as pltpu
from jax.sharding import PartitionSpec as P

MESH = pl.DeviceIdType.MESH
F32 = jnp.float32
BF16 = jnp.bfloat16


def layer_norm(values):
    centred = values - jnp.mean(values, axis=-1, keepdims=True)
    variance = jnp.mean(centred * centred, axis=-1, keepdims=True)
    return centred * lax.rsqrt(variance + 1e-05)


def pick_tile(rows, choices):
    for choice in choices:
        if rows % choice == 0:
            return choice
    return rows


def gather_kernel(
    sizes, x_ref, ent_ref, part_hbm, sharp_hbm, ex_ref, up_ref, dn_ref,
    w_ref, red_ref, exg_ref, upg_ref, dng_ref,
    rows_buf, ent_buf, entt_buf, logit_mat, num_buf, mass_buf,
    piece_all, piece_in, piece_sum, ring_in, fin_buf, part_ref, sharp_ref,
    x_sem, own_sem, zs_sem, zr_sem, fs_sem, fr_sem, cs_sem, cr_sem,
    rs_send, rs_recv, z_send, z_recv, ag_send, ag_recv,
):
    pts, wid, share, tile, head, slices, heads = sizes
    p, w = lax.axis_index("pts"), lax.axis_index("wid")
    rows = rows_buf.shape[0]
    tiles = rows // tile
    norm_tile = pick_tile(rows, (704, 256, 128))
    norm_tiles = rows // norm_tile
    chips = share // 2
    group, core = p // share, p % 2
    chip = (p % share) // 2
    member = core * chips + chip

    x_copy = pltpu.make_async_copy(
        x_ref.at[pl.ds(pl.multiple_of(w * rows, rows), rows)], rows_buf, x_sem
    )
    x_copy.start()

    small_copies = [
        pltpu.make_async_copy(part_hbm, part_ref, own_sem.at[0]),
        pltpu.make_async_copy(sharp_hbm, sharp_ref, own_sem.at[1]),
        pltpu.make_async_copy(ent_ref, ent_buf.at[w], own_sem.at[2]),
    ]
    for copy in small_copies:
        copy.start()

    barrier = pltpu.get_barrier_semaphore()
    for d in range(1, wid):
        pl.semaphore_signal(
            barrier, inc=1, device_id=(p, lax.rem(w + d, wid)), device_id_type=MESH
        )
    for d in range(1, pts):
        pl.semaphore_signal(
            barrier, inc=1, device_id=(lax.rem(p + d, pts), w), device_id_type=MESH
        )
    pl.semaphore_wait(barrier, wid - 1 + pts - 1)

    chunk = ex_ref.shape[0]
    ent_part = ent_ref.shape[0] // share
    out_part = chunk // share

    def spot(m, owner, part, parts=1):
        if m == 0:
            count = ent_part * parts
            return ent_buf.at[owner, pl.ds(pl.multiple_of(part * count, count), count)]
        count = out_part * parts
        full = (exg_ref, upg_ref, dng_ref)[m - 1]
        return full.at[pl.ds(pl.multiple_of(owner * chunk + part * count, count), count)]

    def mine(m):
        if m == 0:
            return spot(0, w, member)
        own = (ex_ref, up_ref, dn_ref)[m - 1]
        return own.at[pl.ds(pl.multiple_of(member * out_part, out_part), out_part)]

    def across(m, d):
        return pltpu.make_async_remote_copy(
            src_ref=mine(m), dst_ref=spot(m, w, member),
            send_sem=zs_sem.at[m, d - 1], recv_sem=zr_sem.at[m, d - 1],
            device_id=(p, lax.rem(w + d, wid)), device_id_type=MESH,
        )

    def forward(m, d, e):
        owner = lax.rem(w - d + wid, wid)
        to = group * share + 2 * lax.rem(chip + e, chips) + core
        return pltpu.make_async_remote_copy(
            src_ref=spot(m, owner, member), dst_ref=spot(m, owner, member),
            send_sem=fs_sem.at[m, d - 1, e - 1], recv_sem=fr_sem.at[m, d - 1, e - 1],
            device_id=(to, w), device_id_type=MESH,
        )

    def swap(m, d):
        owner = lax.rem(w - d + wid, wid)
        half = spot(m, owner, core, chips)
        return pltpu.make_async_remote_copy(
            src_ref=half, dst_ref=half,
            send_sem=cs_sem.at[m, d - 1], recv_sem=cr_sem.at[m, d - 1],
            device_id=(p + 1 - 2 * core, w), device_id_type=MESH,
        )

    small_copies[2].wait()
    crossing = [[across(m, d) for d in range(1, wid)] for m in range(4)]
    for m in range(4):
        for copy in crossing[m]:
            copy.start()
    own_copies = []
    for m in range(1, 4):
        full = (exg_ref, upg_ref, dng_ref)[m - 1]
        copy = pltpu.make_async_copy(
            (ex_ref, up_ref, dn_ref)[m - 1],
            full.at[pl.ds(pl.multiple_of(w * chunk, chunk), chunk)], own_sem.at[m + 2],
        )
        copy.start()
        own_copies.append(copy)

    held = logit_mat.shape[1] // head
    wide = held * slices
    logit_mat[...] = jnp.zeros_like(logit_mat)
    for copy in small_copies[:2]:
        copy.wait()
    part_t = part_ref[...].astype(F32)
    sharp = sharp_ref[...]
    sharp_hi = sharp.astype(BF16).astype(F32)
    sharp_lo = sharp - sharp_hi
    for h in range(held):
        lanes = slice(h * head, (h + 1) * head)
        logit_mat[h * slices:(h + 1) * slices, lanes] = part_t
        logit_mat[wide + h:wide + h + 1, lanes] = sharp_hi
        logit_mat[wide + 8 + h:wide + 8 + h + 1, lanes] = sharp_lo
    num_buf[...] = jnp.zeros_like(num_buf)
    mass_buf[...] = jnp.zeros_like(mass_buf)
    x_copy.wait()

    def norm_step(t, carry):
        at = pl.ds(pl.multiple_of(t * norm_tile, norm_tile), norm_tile)
        rows_buf[at, :] = layer_norm(rows_buf[at, :].astype(F32)).astype(BF16)
        return carry

    norm_way = norm_tiles // 2
    lax.fori_loop(0, norm_way, norm_step, 0)

    def pass_on(m):
        copies = []
        for d in range(1, wid):
            crossing[m][d - 1].wait_recv()
            for e in range(1, chips):
                copy = forward(m, d, e)
                copy.start()
                copies.append(copy)
        return copies

    def trade(m):
        copies = []
        for d in range(1, wid):
            for e in range(1, chips):
                passed[m][(d - 1) * (chips - 1) + e - 1].wait_recv()
            copy = swap(m, d)
            copy.start()
            copies.append(copy)
        return copies

    width = ent_ref.shape[1]
    passed = [pass_on(0)]
    lax.fori_loop(norm_way, norm_tiles, norm_step, 0)
    traded = [trade(0)]
    passed += [pass_on(m) for m in range(1, 4)]
    for copy in traded[0]:
        copy.wait_recv()
    for d in range(wid):
        owner = lax.rem(w - d + wid, wid)
        entt_buf[pl.ds(pl.multiple_of(owner * width, width), width), :] = ent_buf[owner].T

    lhs = logit_mat[...].astype(BF16)
    groups = heads // held
    both = (((1,), (1,)), ((), ()))

    def slice_step(t, carry):
        at = pl.ds(pl.multiple_of(t * tile, tile), tile)
        feats = lax.dot_general(
            entt_buf[...], rows_buf[at, :], both, preferred_element_type=F32
        ).astype(BF16)
        for gi in range(groups):
            own = feats[gi * held * head:(gi + 1) * held * head]
            logits = jnp.dot(lhs, own, preferred_element_type=F32)
            raw = logits[wide:wide + 8] + logits[wide + 8:wide + 16]
            soft = jnp.maximum(raw, 0.0) + jnp.log1p(jnp.exp(-jnp.abs(raw)))
            inverse = 1.0 / (0.5 + soft)
            weights = []
            for h in range(held):
                score = logits[h * slices:(h + 1) * slices] * inverse[h:h + 1]
                power = jnp.exp(score - jnp.max(score, axis=0, keepdims=True))
                weights.append(power * (1.0 / jnp.sum(power, axis=0, keepdims=True)))
            block = jnp.concatenate(weights, axis=0).astype(BF16)
            num_buf[gi] += lax.dot_general(block, own, both, preferred_element_type=F32)
            rounded = block.astype(F32)
            mass = rounded[:, :128]
            for c in range(1, tile // 128):
                mass = mass + rounded[:, c * 128:(c + 1) * 128]
            mass_buf[gi * wide:(gi + 1) * wide] += mass
            w_ref[at, gi * wide:(gi + 1) * wide] = block.T
        return carry

    part_way = (tiles + 1) // 2
    lax.fori_loop(0, part_way, slice_step, 0)
    traded += [trade(m) for m in range(1, 4)]
    lax.fori_loop(part_way, tiles, slice_step, 0)

    lane = lax.broadcasted_iota(jnp.int32, (slices, 2 * head), 1)
    for h in range(heads):
        gi, k = h // held, h % held
        block = num_buf[gi, k * slices:(k + 1) * slices, (k // 2) * 2 * head:(k // 2 + 1) * 2 * head]
        if k % 2:
            block = pltpu.roll(block, head, 1)
        mass = jnp.sum(mass_buf[h * slices:(h + 1) * slices], axis=1, keepdims=True)
        piece_all[h * slices:(h + 1) * slices] = jnp.where(lane < head, block, mass)

    size = heads * slices // pts

    def piece(ref, owner):
        return ref.at[pl.ds(pl.multiple_of(owner * size, size), size)]

    scatter = []
    for d in range(1, pts):
        to = lax.rem(p + d, pts)
        scatter.append(pltpu.make_async_remote_copy(
            src_ref=piece(piece_all, to), dst_ref=piece_in.at[d - 1],
            send_sem=rs_send.at[d - 1], recv_sem=rs_recv.at[d - 1],
            device_id=(to, w), device_id_type=MESH,
        ))
    for copy in scatter:
        copy.start()
    total = piece_all[pl.ds(pl.multiple_of(p * size, size), size)]
    for d in range(1, pts):
        scatter[d - 1].wait_recv()
        total = total + piece_in[d - 1]
    piece_sum[...] = total
    ring = []
    for d in range(1, wid):
        ring.append(pltpu.make_async_remote_copy(
            src_ref=piece_sum, dst_ref=ring_in.at[d - 1],
            send_sem=z_send.at[d - 1], recv_sem=z_recv.at[d - 1],
            device_id=(p, lax.rem(w + d, wid)), device_id_type=MESH,
        ))
    for copy in ring:
        copy.start()
    for d in range(1, wid):
        ring[d - 1].wait_recv()
        total = total + ring_in[d - 1]
    fin_buf[pl.ds(pl.multiple_of(p * size, size), size)] = total
    spread = []
    for d in range(1, pts):
        spread.append(pltpu.make_async_remote_copy(
            src_ref=piece(fin_buf, p), dst_ref=piece(fin_buf, p),
            send_sem=ag_send.at[d - 1], recv_sem=ag_recv.at[d - 1],
            device_id=(lax.rem(p + d, pts), w), device_id_type=MESH,
        ))
    for copy in spread:
        copy.start()
    for copy in spread:
        copy.wait_recv()
    red_ref[...] = fin_buf[...]
    for m in range(1, 4):
        for copy in traded[m]:
            copy.wait_recv()
    for copy in own_copies:
        copy.wait()
    for copies in crossing + passed + traded + [scatter, ring, spread]:
        for copy in copies:
            copy.wait_send()


def rows_kernel(
    sizes, at_ref, red_ref, qkv_ref, w_ref, x_ref, exg_ref, upg_ref, dng_ref, out_ref, mix_buf
):
    head, slices, heads = sizes

    @pl.when(pl.program_id(0) == 0)
    def _():
        high = lax.Precision.HIGHEST
        count = heads * slices
        red = red_ref[...]
        tokens = red[:, :head] / (red[:, head:] + 1e-05)
        queries, keys_all, value_rows = (
            jnp.dot(tokens, qkv_ref[i], precision=high, preferred_element_type=F32)
            for i in range(3)
        )
        scores = lax.dot_general(
            queries, keys_all, (((1,), (1,)), ((), ())), precision=high,
            preferred_element_type=F32,
        ) * (1.0 / head ** 0.5)
        row = lax.broadcasted_iota(jnp.int32, (count, count), 0) // slices
        col = lax.broadcasted_iota(jnp.int32, (count, count), 1) // slices
        scores = jnp.where(row == col, scores, -jnp.inf)
        power = jnp.exp(scores - jnp.max(scores, axis=1, keepdims=True))
        attend = power / jnp.sum(power, axis=1, keepdims=True)
        out_tok = jnp.dot(attend, value_rows, precision=high, preferred_element_type=F32)
        spread = jnp.concatenate([out_tok] * heads, axis=1)
        row = lax.broadcasted_iota(jnp.int32, spread.shape, 0) // slices
        col = lax.broadcasted_iota(jnp.int32, spread.shape, 1) // head
        spread = jnp.where(row == col, spread, 0.0).astype(BF16)
        mix_buf[...] = jnp.dot(
            spread, exg_ref[...], preferred_element_type=F32
        ).astype(BF16)

    midway = x_ref[...].astype(F32) + jnp.dot(
        w_ref[...], mix_buf[...], preferred_element_type=F32
    )
    normed = layer_norm(midway).astype(BF16)
    hidden = jax.nn.gelu(jnp.dot(normed, upg_ref[...], preferred_element_type=F32)).astype(BF16)
    out_ref[...] = (
        midway + jnp.dot(hidden, dng_ref[...], preferred_element_type=F32)
    ).astype(BF16)


def local(x, entry, partition, sharpness, qkv, exit_m, widening, narrowing):
    pts, wid = lax.axis_size("pts"), lax.axis_size("wid")
    width = x.shape[1]
    head, slices = partition.shape
    heads = entry.shape[1] * wid // head
    rows = x.shape[0] // wid
    chunk = exit_m.shape[0]
    cells = heads * slices
    tile = pick_tile(rows, (1408, 256, 128))
    held = 256 // head
    size = cells // pts
    share = 2
    for choice in (8, 4):
        if pts % choice == 0 and chunk % (16 * choice) == 0:
            share = choice
            break
    sizes = (pts, wid, share, tile, head, slices, heads)
    vmem = pl.BlockSpec(memory_space=pltpu.VMEM)
    hbm = pl.BlockSpec(memory_space=pltpu.HBM)
    anywhere = pl.BlockSpec(memory_space=pl.ANY)
    dma = pltpu.SemaphoreType.DMA
    full = jax.ShapeDtypeStruct((chunk * wid, width), BF16)
    weights, reduced, exg, upg, dng = pl.pallas_call(
        functools.partial(gather_kernel, sizes),
        name="slices_and_gather",
        out_shape=(
            jax.ShapeDtypeStruct((rows, cells), BF16),
            jax.ShapeDtypeStruct((cells, 2 * head), F32),
            full, full, full,
        ),
        in_specs=[hbm] * 7,
        out_specs=(vmem, vmem, anywhere, anywhere, anywhere),
        scratch_shapes=[
            pltpu.VMEM((rows, width), BF16),
            pltpu.VMEM((wid,) + entry.shape, BF16),
            pltpu.VMEM((entry.shape[1] * wid, entry.shape[0]), BF16),
            pltpu.VMEM((held * slices + 16, held * head), F32),
            pltpu.VMEM((heads // held, held * slices, held * head), F32),
            pltpu.VMEM((cells, 128), F32),
            pltpu.VMEM((cells, 2 * head), F32),
            pltpu.VMEM((pts - 1, size, 2 * head), F32),
            pltpu.VMEM((size, 2 * head), F32),
            pltpu.VMEM((wid - 1, size, 2 * head), F32),
            pltpu.VMEM((cells, 2 * head), F32),
            pltpu.VMEM((slices, head), BF16),
            pltpu.VMEM((1, head), F32),
            dma, dma((6,)),
            dma((4, wid - 1)), dma((4, wid - 1)),
            dma((4, wid - 1, max(share // 2 - 1, 1))), dma((4, wid - 1, max(share // 2 - 1, 1))),
            dma((4, wid - 1)), dma((4, wid - 1)),
            dma((pts - 1,)), dma((pts - 1,)),
            dma((wid - 1,)), dma((wid - 1,)),
            dma((pts - 1,)), dma((pts - 1,)),
        ],
        compiler_params=pltpu.CompilerParams(
            collective_id=0, has_side_effects=True, vmem_limit_bytes=60 * 1024 * 1024
        ),
    )(x, entry, partition.T, sharpness.reshape(1, head), exit_m, widening, narrowing)

    step = pick_tile(rows, (1408, 704, 256, 128))
    steps = rows // step
    whole = lambda a: pl.BlockSpec(a.shape, lambda i, at: (0,) * a.ndim)
    at = lax.axis_index("wid").astype(jnp.int32).reshape(1)
    return pl.pallas_call(
        functools.partial(rows_kernel, (head, slices, heads)),
        name="mix_and_feed",
        out_shape=jax.ShapeDtypeStruct((rows, width), BF16),
        grid_spec=pltpu.PrefetchScalarGridSpec(
            num_scalar_prefetch=1,
            grid=(steps,),
            in_specs=[
                whole(reduced),
                whole(qkv),
                pl.BlockSpec((step, cells), lambda i, at: (i, 0)),
                pl.BlockSpec((step, width), lambda i, at: (at[0] * steps + i, 0)),
                whole(exg), whole(upg), whole(dng),
            ],
            out_specs=pl.BlockSpec((step, width), lambda i, at: (i, 0)),
            scratch_shapes=[pltpu.VMEM((cells, width), BF16)],
        ),
        compiler_params=pltpu.CompilerParams(
            dimension_semantics=("arbitrary",), vmem_limit_bytes=61 * 1024 * 1024
        ),
    )(at, reduced, qkv, weights, x, exg, upg, dng)


def solution(mesh):
    placed = (
        P("pts", None),
        P(None, "wid"),
        P(),
        P(),
        P(),
        P("wid", None),
        P("wid", None),
        P("wid", None),
    )
    return jax.shard_map(
        local, mesh=mesh, in_specs=placed, out_specs=P(("pts", "wid"), None), check_vma=False
    )
```

profile of v0, /device:TPU:0, one launch (start us, length us, event | category | flops | bytes accessed | tf_op | source)
XLA Modules:
  0.0 46.6 jit_solution(12244394268707064452)
XLA Ops:
  0.0 35.9 %slices_and_gather.1 = (bf16[2816,256]{1,0:T(8,128)(2,1)}, f32[256,128]{1,0:T(8,128)}, bf16[512,512]{1,0:T(8,128)(2,1)}, bf16[512,512]{1,0:T(8,128)(2,1)}, bf16[512,512]{1,0:T(8,128)(2,1)}) custom-call(bf16[11264,512]{1,0:T(8,128)(2,1)} %x_ref.3, bf16[512,128]{1,0:T(8,128)(2,1)} %ent_ref.1, bf16[32,64]{1,0:T(8,128)(2,1)} %bitcast.3, f32[1,64]{1,0:T(1,128)} %bitcast.4, ...), custom_call_target="tpu_custom_call" | custom-call | tf_op jit(solution)/shard_map/slices_and_gather/pallas_call | solution.py:350
  36.0 10.7 %mix_and_feed.1 = bf16[2816,512]{1,0:T(8,128)(2,1)} custom-call(s32[1]{0:T(128)} %bitcast.at_ref, f32[256,128]{1,0:T(8,128)} %get-tuple-element.10.red_ref, f32[3,64,64]{2,1,0:T(8,128)} %qkv_ref.1, bf16[2816,256]{1,0:T(8,128)(2,1)} %get-tuple-element.11.w_ref, bf16[11264,512]{1,0:T(8,128)(2,1)} %x_ref.3, bf16[512,512]{1,0:T(8,128)(2,1)} %get-tuple-element.12.exg_ref, ...), custom_call_target="tpu_custom_call" | custom-call | tf_op jit(solution)/shard_map/mix_and_feed/pallas_call | solution.py:391
where the time goes:
time: 46.8 us; the launch traced here: 46.6 us
  Pallas kernels  46.6 us (100%)
    pallas_call x1, Pallas kernels, local(): pl.pallas_call(functools.partial(gather_kernel, sizes), name='slices_and_...  35.9 us
    pallas_call x1, Pallas kernels, local(): pl.pallas_call(functools.partial(rows_kernel, (head, slices, heads)), nam...  10.7 us

commit v1 on v0

v1 whole, which is shorter than its diff:
```python
import functools
import math

import jax
import jax.numpy as jnp
from jax import lax
from jax.experimental import pallas as pl
from jax.experimental.pallas import tpu as pltpu
from jax.sharding import PartitionSpec as P

MESH = pl.DeviceIdType.MESH
F32 = jnp.float32
BF16 = jnp.bfloat16
HIGH = lax.Precision.HIGHEST
LOG2E = math.log2(math.e)
BOTH = (((1,), (1,)), ((), ()))


def layer_norm(values):
    centred = values - jnp.mean(values, axis=-1, keepdims=True)
    variance = jnp.mean(centred * centred, axis=-1, keepdims=True)
    return centred * lax.rsqrt(variance + 1e-05)


def pick_tile(rows, choices):
    for choice in choices:
        if rows % choice == 0:
            return choice
    return rows


def fold_rows(values, held, combine):
    shift = 4
    while shift >= held:
        values = combine(values, pltpu.roll(values, shift, 0))
        shift //= 2
    return values


def slice_softmax(logits, held, slices):
    wide = held * slices
    raw = logits[wide:wide + 8] + logits[wide + 8:wide + 16]
    soft = jnp.maximum(raw, 0.0) + jnp.log1p(jnp.exp(-jnp.abs(raw)))
    inverse = LOG2E / (0.5 + soft)
    score = logits[:wide].reshape(wide // 8, 8, logits.shape[1]) * inverse[None]
    top = fold_rows(jnp.max(score, axis=0), held, jnp.maximum)
    power = jnp.exp2(score - top[None])
    total = fold_rows(jnp.sum(power, axis=0), held, jnp.add)
    return (power * (1.0 / total)[None]).reshape(wide, logits.shape[1]).astype(BF16)


def fill_logit_mat(mat, part_t, sharp, held, slices, head):
    wide = held * slices
    sharp_hi = sharp.astype(BF16).astype(F32)
    sharp_lo = sharp - sharp_hi
    shape = (wide, head)
    row = lax.broadcasted_iota(jnp.int32, (wide, slices), 0) // held
    col = lax.broadcasted_iota(jnp.int32, (wide, slices), 1)
    pick = jnp.where(row == col, 1.0, 0.0).astype(BF16)
    spread = jnp.dot(pick, part_t, preferred_element_type=F32)
    which = lax.broadcasted_iota(jnp.int32, shape, 0) % held
    small = lax.broadcasted_iota(jnp.int32, (8, head), 0) % held
    for h in range(held):
        lanes = slice(h * head, (h + 1) * head)
        mat[:wide, lanes] = jnp.where(which == h, spread, 0.0)
        mat[wide:wide + 8, lanes] = jnp.where(small == h, sharp_hi, 0.0)
        mat[wide + 8:wide + 16, lanes] = jnp.where(small == h, sharp_lo, 0.0)


def gather_kernel(
    sizes, x_ref, ent_ref, part_hbm, sharp_hbm, qkv_hbm, ex_ref, up_ref, dn_ref,
    w_ref, mix_ref, xo_ref, upg_ref, dng_ref,
    x_all, rows_buf, ent_buf, ext_buf, entt_buf, exg_ref, local_mat, all_mat, num_buf, mass_buf,
    piece_out, piece_in, qkv_ref, big_qkv, tok_buf, part_ref, sharp_ref,
    x_sem, own_sem, zs_sem, zr_sem, fs_sem, fr_sem, cs_sem, cr_sem,
    a_send, a_recv, t_send, t_recv,
):
    pts, wid, share, step, tile, head, slices, heads = sizes
    p, w = lax.axis_index("pts"), lax.axis_index("wid")
    total_rows, model = x_all.shape
    rows = rows_buf.shape[0]
    steps = total_rows // step
    tiles = rows // tile
    chips = share // 2
    group, core = p // share, p % 2
    chip = (p % share) // 2
    member = core * chips + chip
    mine_heads = heads // wid
    local_lanes = mine_heads * head
    local_wide = mine_heads * slices
    held = all_mat.shape[1] // head
    wide = held * slices
    groups = heads // held
    chunk = ex_ref.shape[0]

    def x_copy(t):
        at = pl.ds(pl.multiple_of(t * step, step), step)
        return pltpu.make_async_copy(x_ref.at[at], x_all.at[at], x_sem.at[t])

    small_copies = [
        pltpu.make_async_copy(ent_ref, ent_buf.at[w], own_sem.at[0]),
        pltpu.make_async_copy(part_hbm, part_ref, own_sem.at[1]),
        pltpu.make_async_copy(sharp_hbm, sharp_ref, own_sem.at[2]),
        pltpu.make_async_copy(qkv_hbm, qkv_ref, own_sem.at[3]),
    ]
    for copy in small_copies[:3]:
        copy.start()
    x_copy(0).start()
    own_copies = []
    for m in range(1, 4):
        full = (exg_ref, upg_ref, dng_ref)[m - 1]
        own_copies.append(pltpu.make_async_copy(
            (ex_ref, up_ref, dn_ref)[m - 1],
            full.at[pl.ds(pl.multiple_of(w * chunk, chunk), chunk)], own_sem.at[m + 3],
        ))
    for copy in own_copies:
        copy.start()
    for t in range(1, steps):
        x_copy(t).start()
    small_copies[3].start()
    own_rows = pltpu.make_async_copy(
        x_ref.at[pl.ds(pl.multiple_of(w * rows, rows), rows)], xo_ref, own_sem.at[7]
    )
    own_rows.start()

    barrier = pltpu.get_barrier_semaphore()
    for d in range(1, wid):
        pl.semaphore_signal(
            barrier, inc=1, device_id=(p, lax.rem(w + d, wid)), device_id_type=MESH
        )
    for d in range(1, pts):
        pl.semaphore_signal(
            barrier, inc=1, device_id=(lax.rem(p + d, pts), w), device_id_type=MESH
        )

    ent_part = ent_ref.shape[0] // share
    out_part = chunk // share

    def spot(m, owner, part, parts=1):
        if m == 0:
            count = ent_part * parts
            return ent_buf.at[owner, pl.ds(pl.multiple_of(part * count, count), count)]
        count = out_part * parts
        full = (exg_ref, upg_ref, dng_ref)[m - 1]
        return full.at[pl.ds(pl.multiple_of(owner * chunk + part * count, count), count)]

    def across(m, d):
        return pltpu.make_async_remote_copy(
            src_ref=spot(m, w, member), dst_ref=spot(m, w, member),
            send_sem=zs_sem.at[m, d - 1], recv_sem=zr_sem.at[m, d - 1],
            device_id=(p, lax.rem(w + d, wid)), device_id_type=MESH,
        )

    def forward(m, d, e):
        owner = lax.rem(w - d + wid, wid)
        to = group * share + 2 * lax.rem(chip + e, chips) + core
        return pltpu.make_async_remote_copy(
            src_ref=spot(m, owner, member), dst_ref=spot(m, owner, member),
            send_sem=fs_sem.at[m, d - 1, e - 1], recv_sem=fr_sem.at[m, d - 1, e - 1],
            device_id=(to, w), device_id_type=MESH,
        )

    def swap(m, d):
        owner = lax.rem(w - d + wid, wid)
        half = spot(m, owner, core, chips)
        return pltpu.make_async_remote_copy(
            src_ref=half, dst_ref=half,
            send_sem=cs_sem.at[m, d - 1], recv_sem=cr_sem.at[m, d - 1],
            device_id=(p + 1 - 2 * core, w), device_id_type=MESH,
        )

    def cross_all():
        for m in range(4):
            for d in range(1, wid):
                across(m, d).start()

    def pass_on(m):
        for d in range(1, wid):
            across(m, d).wait_recv()
            for e in range(1, chips):
                forward(m, d, e).start()

    def trade(m):
        for d in range(1, wid):
            for e in range(1, chips):
                forward(m, d, e).wait_recv()
            swap(m, d).start()

    def traded(m):
        for d in range(1, wid):
            swap(m, d).wait_recv()

    ext_buf[...] = jnp.zeros_like(ext_buf)
    ext_buf[:, 128:] = jnp.ones((model, 128), BF16)
    piece_out[...] = jnp.zeros_like(piece_out)
    num_buf[...] = jnp.zeros_like(num_buf)
    mass_buf[...] = jnp.zeros_like(mass_buf)
    local_mat[...] = jnp.zeros_like(local_mat)
    all_mat[...] = jnp.zeros_like(all_mat)
    big_qkv[...] = jnp.zeros_like(big_qkv)
    tok_buf[...] = jnp.zeros_like(tok_buf)
    for copy in small_copies[:3]:
        copy.wait()
    part_t, sharp = part_ref[...], sharp_ref[...]
    fill_logit_mat(local_mat, part_t, sharp, mine_heads, slices, head)
    fill_logit_mat(all_mat, part_t, sharp, held, slices, head)
    ext_buf[:, :local_lanes] = ent_buf[w]
    column_sum = jnp.sum(ext_buf[:, :128].astype(F32), axis=0, keepdims=True)
    local_lhs = local_mat[...].astype(BF16)

    def numerator_step(t, carry):
        @pl.when(t == 1)
        def _():
            pl.semaphore_wait(barrier, wid - 1 + pts - 1)
            for copy in own_copies:
                copy.wait()
            cross_all()

        @pl.when(t == steps - 2)
        def _():
            pass_on(0)

        x_copy(t).wait()
        at = pl.ds(pl.multiple_of(t * step, step), step)
        narrow = x_all[at, :]
        raw = jnp.dot(narrow, ext_buf[...], preferred_element_type=F32)
        mean = raw[:, 128:] * (1.0 / model)
        wider = narrow.astype(F32)
        centred = wider - jnp.concatenate([mean] * (model // 128), axis=1)
        variance = jnp.sum(centred * centred, axis=1, keepdims=True) * (1.0 / model)
        feats = ((raw[:, :128] - mean * column_sum) * lax.rsqrt(variance + 1e-05)).astype(BF16)
        logits = lax.dot_general(local_lhs, feats, BOTH, preferred_element_type=F32)
        block = slice_softmax(logits, mine_heads, slices)
        num_buf[...] += jnp.dot(block, feats, preferred_element_type=F32)
        rounded = block.astype(F32)
        mass = rounded[:, :128]
        for c in range(1, step // 128):
            mass = mass + rounded[:, c * 128:(c + 1) * 128]
        mass_buf[...] += mass
        return carry

    lax.fori_loop(0, steps, numerator_step, 0)

    lane = lax.broadcasted_iota(jnp.int32, (slices, 128), 1)
    packed = jnp.zeros((slices, 128), F32)
    for h in range(mine_heads):
        packed = jnp.where(lane // head == h, num_buf[pl.ds(h, slices, stride=mine_heads), :], packed)
    piece_out[:slices, :] = packed
    piece_out[slices:, :local_wide] = lax.dot_general(
        jnp.ones((8, 128), F32), mass_buf[...], BOTH, precision=HIGH, preferred_element_type=F32
    )
    spread = []
    for d in range(1, pts):
        spread.append(pltpu.make_async_remote_copy(
            src_ref=piece_out, dst_ref=piece_in.at[d - 1],
            send_sem=a_send.at[d - 1], recv_sem=a_recv.at[d - 1],
            device_id=(lax.rem(p + d, pts), w), device_id_type=MESH,
        ))
    for copy in spread:
        copy.start()

    for m in range(1, 4):
        pass_on(m)
    small_copies[3].wait()
    for i in range(3):
        for h in range(mine_heads):
            at = slice(h * head, (h + 1) * head)
            big_qkv[i, at, at] = qkv_ref[i]

    own_rows.wait()
    norm_tile = pick_tile(rows, (704, 256, 128))

    def norm_step(t, carry):
        at = pl.ds(pl.multiple_of(t * norm_tile, norm_tile), norm_tile)
        rows_buf[at, :] = layer_norm(xo_ref[at, :].astype(F32)).astype(BF16)
        return carry

    lax.fori_loop(0, rows // norm_tile, norm_step, 0)
    trade(0)

    total = piece_out[...]
    for d in range(1, pts):
        spread[d - 1].wait_recv()
        total = total + piece_in[d - 1]
    row = lax.broadcasted_iota(jnp.int32, (slices, local_wide), 0)
    col = lax.broadcasted_iota(jnp.int32, (slices, local_wide), 1)
    masses = jnp.ones((slices, 128), F32)
    for h in range(mine_heads):
        one = jnp.sum(
            jnp.where(col == row * mine_heads + h, total[slices:slices + 1, :local_wide], 0.0),
            axis=1, keepdims=True,
        )
        masses = jnp.where(lane // head == h, one, masses)
    tokens = total[:slices] / (masses + 1e-05)
    queries, keys_all, value_rows = (
        jnp.dot(tokens, big_qkv[i], precision=HIGH, preferred_element_type=F32) for i in range(3)
    )
    stacked = lambda a: jnp.concatenate(
        [jnp.where(lane // head == h, a, 0.0) for h in range(mine_heads)], axis=0
    )
    scores = lax.dot_general(
        queries, stacked(keys_all), BOTH, precision=HIGH, preferred_element_type=F32
    ) * (1.0 / head ** 0.5)
    owner_head = col // slices
    attend = jnp.zeros_like(scores)
    for h in range(mine_heads):
        part = jnp.where(owner_head == h, scores, -jnp.inf)
        power = jnp.exp(part - jnp.max(part, axis=1, keepdims=True))
        attend = attend + power / jnp.sum(power, axis=1, keepdims=True)
    tok_buf[w] = jnp.dot(
        attend, stacked(value_rows), precision=HIGH, preferred_element_type=F32
    ).astype(BF16)
    ring = []
    for d in range(1, wid):
        ring.append(pltpu.make_async_remote_copy(
            src_ref=tok_buf.at[w], dst_ref=tok_buf.at[w],
            send_sem=t_send.at[d - 1], recv_sem=t_recv.at[d - 1],
            device_id=(p, lax.rem(w + d, wid)), device_id_type=MESH,
        ))
    for copy in ring:
        copy.start()

    traded(0)
    trade(1)
    width = ent_ref.shape[1]
    for owner in range(wid):
        entt_buf[owner * width:(owner + 1) * width, :] = ent_buf[owner].T
    lhs = all_mat[...].astype(BF16)

    def slice_step(t, carry):
        at = pl.ds(pl.multiple_of(t * tile, tile), tile)
        feats = lax.dot_general(
            entt_buf[...], rows_buf[at, :], BOTH, preferred_element_type=F32
        ).astype(BF16)
        for gi in range(groups):
            own = feats[gi * held * head:(gi + 1) * held * head]
            logits = jnp.dot(lhs, own, preferred_element_type=F32)
            w_ref[at, gi * wide:(gi + 1) * wide] = slice_softmax(logits, held, slices).T
        return carry

    lax.fori_loop(0, tiles, slice_step, 0)
    for m in range(2, 4):
        trade(m)
    traded(1)
    for copy in ring:
        copy.wait_recv()

    row = lax.broadcasted_iota(jnp.int32, (wide, slices), 0) // held
    col = lax.broadcasted_iota(jnp.int32, (wide, slices), 1)
    repeat = jnp.where(row == col, 1.0, 0.0).astype(BF16)
    row = lax.broadcasted_iota(jnp.int32, (wide, held * head), 0) % held
    col = lax.broadcasted_iota(jnp.int32, (wide, held * head), 1) // head
    every = jnp.concatenate(
        [tok_buf[z].astype(F32)[:, :local_lanes] for z in range(wid)], axis=1
    ).astype(BF16)
    for gi in range(groups):
        lanes = slice(gi * held * head, (gi + 1) * held * head)
        block = jnp.dot(repeat, every[:, lanes], preferred_element_type=F32)
        block = jnp.where(row == col, block, 0.0).astype(BF16)
        mix_ref[gi * wide:(gi + 1) * wide, :] = jnp.dot(
            block, exg_ref[lanes, :], preferred_element_type=F32
        ).astype(BF16)
    for m in range(2, 4):
        traded(m)
    for m in range(4):
        for d in range(1, wid):
            across(m, d).wait_send()
            swap(m, d).wait_send()
            for e in range(1, chips):
                forward(m, d, e).wait_send()
    for copy in spread + ring:
        copy.wait_send()


def rows_kernel(step, w_ref, mix_ref, x_ref, upg_ref, dng_ref, out_ref, out_buf, out_sem):
    steps = x_ref.shape[0] // step

    def out_copy(t, slot):
        at = pl.ds(pl.multiple_of(t * step, step), step)
        return pltpu.make_async_copy(out_buf.at[slot], out_ref.at[at], out_sem.at[slot])

    def feed_step(t, carry):
        slot = lax.rem(t, 2)
        at = pl.ds(pl.multiple_of(t * step, step), step)
        midway = x_ref[at, :].astype(F32) + jnp.dot(
            w_ref[at, :], mix_ref[...], preferred_element_type=F32
        )
        normed = layer_norm(midway).astype(BF16)
        hidden = jax.nn.gelu(
            jnp.dot(normed, upg_ref[...], preferred_element_type=F32)
        ).astype(BF16)
        result = (
            midway + jnp.dot(hidden, dng_ref[...], preferred_element_type=F32)
        ).astype(BF16)

        @pl.when(t >= 2)
        def _():
            out_copy(t - 2, slot).wait()

        out_buf[slot] = result
        out_copy(t, slot).start()
        return carry

    lax.fori_loop(0, steps, feed_step, 0)
    for t in range(max(steps - 2, 0), steps):
        out_copy(t, t % 2).wait()


def local(x, entry, partition, sharpness, qkv, exit_m, widening, narrowing):
    pts, wid = lax.axis_size("pts"), lax.axis_size("wid")
    width = x.shape[1]
    head, slices = partition.shape
    heads = entry.shape[1] * wid // head
    mine = heads // wid
    rows = x.shape[0] // wid
    chunk = exit_m.shape[0]
    cells = heads * slices
    step = pick_tile(x.shape[0], (1408, 1024, 512, 256, 128))
    tile = pick_tile(rows, (1408, 256, 128))
    held = 256 // head
    share = 2
    for choice in (8, 4):
        if pts % choice == 0 and chunk % (16 * choice) == 0:
            share = choice
            break
    sizes = (pts, wid, share, step, tile, head, slices, heads)
    vmem = pl.BlockSpec(memory_space=pltpu.VMEM)
    hbm = pl.BlockSpec(memory_space=pltpu.HBM)
    dma = pltpu.SemaphoreType.DMA
    full = pltpu.VMEM((chunk * wid, width), BF16)
    hops = max(share // 2 - 1, 1)
    x = pltpu.with_memory_space_constraint(x, pltpu.HBM)
    weights, mix, own, upg, dng = pl.pallas_call(
        functools.partial(gather_kernel, sizes),
        name="slices_and_gather",
        out_shape=(
            pltpu.VMEM((rows, cells), BF16),
            pltpu.VMEM((cells, width), BF16),
            pltpu.VMEM((rows, width), BF16),
            full, full,
        ),
        in_specs=[hbm] * 8,
        out_specs=(vmem,) * 5,
        scratch_shapes=[
            pltpu.VMEM(x.shape, BF16),
            pltpu.VMEM((rows, width), BF16),
            pltpu.VMEM((wid,) + entry.shape, BF16),
            pltpu.VMEM((width, 256), BF16),
            pltpu.VMEM((entry.shape[1] * wid, entry.shape[0]), BF16),
            pltpu.VMEM((chunk * wid, width), BF16),
            pltpu.VMEM((mine * slices + 16, 128), F32),
            pltpu.VMEM((held * slices + 16, held * head), F32),
            pltpu.VMEM((mine * slices, 128), F32),
            pltpu.VMEM((mine * slices, 128), F32),
            pltpu.VMEM((slices + 8, 128), F32),
            pltpu.VMEM((pts - 1, slices + 8, 128), F32),
            pltpu.VMEM(qkv.shape, F32),
            pltpu.VMEM((3, 128, 128), F32),
            pltpu.VMEM((wid, slices, 128), BF16),
            pltpu.VMEM((slices, head), BF16),
            pltpu.VMEM((1, head), F32),
            dma((x.shape[0] // step,)), dma((8,)),
            dma((4, wid - 1)), dma((4, wid - 1)),
            dma((4, wid - 1, hops)), dma((4, wid - 1, hops)),
            dma((4, wid - 1)), dma((4, wid - 1)),
            dma((pts - 1,)), dma((pts - 1,)),
            dma((wid - 1,)), dma((wid - 1,)),
        ],
        compiler_params=pltpu.CompilerParams(
            collective_id=0, has_side_effects=True, vmem_limit_bytes=44 * 1024 * 1024
        ),
    )(x, entry, partition.T, sharpness.reshape(1, head), qkv, exit_m, widening, narrowing)

    step = pick_tile(rows, (704, 256, 128))
    return pl.pallas_call(
        functools.partial(rows_kernel, step),
        name="mix_and_feed",
        out_shape=jax.ShapeDtypeStruct((rows, width), BF16),
        in_specs=[vmem] * 5,
        out_specs=pl.BlockSpec(memory_space=pl.ANY),
        scratch_shapes=[pltpu.VMEM((2, step, width), BF16), dma((2,))],
        compiler_params=pltpu.CompilerParams(vmem_limit_bytes=40 * 1024 * 1024),
    )(weights, mix, own, upg, dng)


def solution(mesh):
    placed = (
        P("pts", None),
        P(None, "wid"),
        P(),
        P(),
        P(),
        P("wid", None),
        P("wid", None),
        P("wid", None),
    )
    return jax.shard_map(
        local, mesh=mesh, in_specs=placed, out_specs=P(("pts", "wid"), None), check_vma=False
    )
```

time: 46.8 us -> 43.6 us (0.932)
  Pallas kernels: 46.6 us -> 37.5 us
  local copies, waits for them, and re-layouts: 0 us -> 5.86 us
    pallas_call x1, Pallas kernels: 35.9 us -> 29.6 us  [local(): pl.pallas_call(functools.partial(gather_kernel, sizes), name='slices_and_...]
    unnamed x0 -> x14, local copies, waits for them, and re-layouts: none -> 5.86 us
    pallas_call x1, Pallas kernels: 10.7 us -> 7.83 us  [local(): pl.pallas_call(functools.partial(rows_kernel, step), name='mix_and_feed',...]
where the time goes in v1:
time: 43.6 us; the launch traced here: 43.3 us
  Pallas kernels  37.5 us (86%)
  local copies, waits for them, and re-layouts  5.86 us (13%)
    pallas_call x1, Pallas kernels, local(): pl.pallas_call(functools.partial(gather_kernel, sizes), name='slices_and_...  29.6 us
    pallas_call x1, Pallas kernels, local(): pl.pallas_call(functools.partial(rows_kernel, step), name='mix_and_feed',...  7.83 us
    unnamed x14, local copies, waits for them, and re-layouts  5.86 us

profile of v1, /device:TPU:0, one launch (start us, length us, event | category | flops | bytes accessed | tf_op | source)
XLA Modules:
  0.0 43.3 jit_solution(9690510915537509720)
XLA Ops:
  0.0 0.0 copy-start
  0.0 0.9 %copy-done = bf16[512,128]{1,0:T(8,128)(2,1)S(1)} copy-done((bf16[512,128]{1,0:T(8,128)(2,1)S(1)}, bf16[512,128]{1,0:T(8,128)(2,1)}, u32[]{:S(2)}) %copy-start) | copy-done | bytes 131096
  0.9 0.0 copy-start.1
  0.9 0.9 %copy-done.1 = bf16[128,512]{1,0:T(8,128)(2,1)S(1)} copy-done((bf16[128,512]{1,0:T(8,128)(2,1)S(1)}, bf16[128,512]{1,0:T(8,128)(2,1)}, u32[]{:S(2)}) %copy-start.1) | copy-done | bytes 131096
  1.8 0.0 copy-start.2
  1.8 0.9 %copy-done.2 = bf16[128,512]{1,0:T(8,128)(2,1)S(1)} copy-done((bf16[128,512]{1,0:T(8,128)(2,1)S(1)}, bf16[128,512]{1,0:T(8,128)(2,1)}, u32[]{:S(2)}) %copy-start.2) | copy-done | bytes 131096
  2.7 0.0 copy-start.3
  2.7 0.9 %copy-done.3 = bf16[128,512]{1,0:T(8,128)(2,1)S(1)} copy-done((bf16[128,512]{1,0:T(8,128)(2,1)S(1)}, bf16[128,512]{1,0:T(8,128)(2,1)}, u32[]{:S(2)}) %copy-start.3) | copy-done | bytes 131096
  3.6 0.0 copy-start.4
  3.6 0.9 %copy-done.4 = f32[3,64,64]{2,1,0:T(8,128)S(1)} copy-done((f32[3,64,64]{2,1,0:T(8,128)S(1)}, f32[3,64,64]{2,1,0:T(8,128)}, u32[]{:S(2)}) %copy-start.4) | copy-done | bytes 49176
  4.5 0.0 copy-start.5
  4.5 0.7 %copy-done.5 = bf16[64,32]{0,1:T(8,128)(2,1)S(1)} copy-done((bf16[64,32]{0,1:T(8,128)(2,1)S(1)}, bf16[64,32]{0,1:T(8,128)(2,1)}, u32[]{:S(2)}) %copy-start.5) | copy-done | bytes 4120
  5.2 0.0 copy-start.6
  5.2 0.7 %copy-done.6 = f32[64]{0:T(128)S(1)} copy-done((f32[64]{0:T(128)S(1)}, f32[64]{0:T(128)}, u32[]{:S(2)}) %copy-start.6) | copy-done | bytes 280
  5.9 29.6 %slices_and_gather.1 = (bf16[2816,256]{1,0:T(8,128)(2,1)S(1)}, bf16[256,512]{1,0:T(8,128)(2,1)S(1)}, bf16[2816,512]{1,0:T(8,128)(2,1)S(1)}, bf16[512,512]{1,0:T(8,128)(2,1)S(1)}, bf16[512,512]{1,0:T(8,128)(2,1)S(1)}) custom-call(bf16[11264,512]{1,0:T(8,128)(2,1)} %x_ref.1, bf16[512,128]{1,0:T(8,128)(2,1)S(1)} %copy-done, bf16[32,64]{1,0:T(8,128)(2,1)S(1)} %bitcast.2, ...), custom_call_target="tpu_custom_call" | custom-call | tf_op jit(solution)/shard_map/slices_and_gather/pallas_call | solution.py:433
  35.5 7.8 %mix_and_feed.1 = bf16[2816,512]{1,0:T(8,128)(2,1)} custom-call(bf16[2816,256]{1,0:T(8,128)(2,1)S(1)} %get-tuple-element.10.w_ref, bf16[256,512]{1,0:T(8,128)(2,1)S(1)} %get-tuple-element.11.mix_ref, bf16[2816,512]{1,0:T(8,128)(2,1)S(1)} %get-tuple-element.12.x_ref, bf16[512,512]{1,0:T(8,128)(2,1)S(1)} %get-tuple-element.13.upg_ref, ...), custom_call_target="tpu_custom_call" | custom-call | tf_op jit(solution)/shard_map/mix_and_feed/pallas_call | solution.py:475
Async XLA Ops:
  0.0 0.9 %copy-start = (bf16[512,128]{1,0:T(8,128)(2,1)S(1)}, bf16[512,128]{1,0:T(8,128)(2,1)}, u32[]{:S(2)}) copy-start(bf16[512,128]{1,0:T(8,128)(2,1)} %ent_ref.1) | copy-start | bytes 393220
  0.9 0.9 %copy-start.1 = (bf16[128,512]{1,0:T(8,128)(2,1)S(1)}, bf16[128,512]{1,0:T(8,128)(2,1)}, u32[]{:S(2)}) copy-start(bf16[128,512]{1,0:T(8,128)(2,1)} %ex_ref.1) | copy-start | bytes 393220
  1.8 0.9 %copy-start.2 = (bf16[128,512]{1,0:T(8,128)(2,1)S(1)}, bf16[128,512]{1,0:T(8,128)(2,1)}, u32[]{:S(2)}) copy-start(bf16[128,512]{1,0:T(8,128)(2,1)} %up_ref.1) | copy-start | bytes 393220
  2.7 0.9 %copy-start.3 = (bf16[128,512]{1,0:T(8,128)(2,1)S(1)}, bf16[128,512]{1,0:T(8,128)(2,1)}, u32[]{:S(2)}) copy-start(bf16[128,512]{1,0:T(8,128)(2,1)} %dn_ref.1) | copy-start | bytes 393220
  3.6 0.9 %copy-start.4 = (f32[3,64,64]{2,1,0:T(8,128)S(1)}, f32[3,64,64]{2,1,0:T(8,128)}, u32[]{:S(2)}) copy-start(f32[3,64,64]{2,1,0:T(8,128)} %qkv_hbm.1) | copy-start | bytes 147460
  4.5 0.7 %copy-start.5 = (bf16[64,32]{0,1:T(8,128)(2,1)S(1)}, bf16[64,32]{0,1:T(8,128)(2,1)}, u32[]{:S(2)}) copy-start(bf16[64,32]{0,1:T(8,128)(2,1)} %param.10) | copy-start | bytes 12292
  5.2 0.7 %copy-start.6 = (f32[64]{0:T(128)S(1)}, f32[64]{0:T(128)}, u32[]{:S(2)}) copy-start(f32[64]{0:T(128)} %param.11) | copy-start | bytes 772

commit v2 on v1

v2 whole, which is shorter than its diff:
```python
import functools
import math

import jax
import jax.numpy as jnp
from jax import lax
from jax.experimental import pallas as pl
from jax.experimental.pallas import tpu as pltpu
from jax.sharding import PartitionSpec as P

MESH = pl.DeviceIdType.MESH
F32 = jnp.float32
BF16 = jnp.bfloat16
HIGH = lax.Precision.HIGHEST
LOG2E = math.log2(math.e)
BOTH = (((1,), (1,)), ((), ()))
GELU_A = math.sqrt(2.0 / math.pi)
GELU_B = 0.044715 * math.sqrt(2.0 / math.pi)


def layer_norm(values):
    centred = values - jnp.mean(values, axis=-1, keepdims=True)
    variance = jnp.mean(centred * centred, axis=-1, keepdims=True)
    return centred * lax.rsqrt(variance + 1e-05)


def pick_tile(rows, choices):
    for choice in choices:
        if rows % choice == 0:
            return choice
    return rows


def fold_rows(values, held, combine):
    shift = 4
    while shift >= held:
        values = combine(values, pltpu.roll(values, shift, 0))
        shift //= 2
    return values


def slice_softmax(logits, held, slices):
    wide = held * slices
    raw = logits[wide:wide + 8] + logits[wide + 8:wide + 16]
    soft = jnp.maximum(raw, 0.0) + jnp.log1p(jnp.exp(-jnp.abs(raw)))
    inverse = LOG2E / (0.5 + soft)
    score = logits[:wide].reshape(wide // 8, 8, logits.shape[1]) * inverse[None]
    top = fold_rows(jnp.max(score, axis=0), held, jnp.maximum)
    power = jnp.exp2(score - top[None])
    total = fold_rows(jnp.sum(power, axis=0), held, jnp.add)
    return (power * (1.0 / total)[None]).reshape(wide, logits.shape[1]).astype(BF16)


def fill_logit_mat(mat, part_t, sharp, held, slices, head):
    wide = held * slices
    sharp_hi = sharp.astype(BF16).astype(F32)
    sharp_lo = sharp - sharp_hi
    shape = (wide, head)
    row = lax.broadcasted_iota(jnp.int32, (wide, slices), 0) // held
    col = lax.broadcasted_iota(jnp.int32, (wide, slices), 1)
    pick = jnp.where(row == col, 1.0, 0.0).astype(BF16)
    spread = jnp.dot(pick, part_t, preferred_element_type=F32)
    which = lax.broadcasted_iota(jnp.int32, shape, 0) % held
    small = lax.broadcasted_iota(jnp.int32, (8, head), 0) % held
    for h in range(held):
        lanes = slice(h * head, (h + 1) * head)
        mat[:wide, lanes] = jnp.where(which == h, spread, 0.0)
        mat[wide:wide + 8, lanes] = jnp.where(small == h, sharp_hi, 0.0)
        mat[wide + 8:wide + 16, lanes] = jnp.where(small == h, sharp_lo, 0.0)


def gather_kernel(
    sizes, x_ref, ent_ref, part_hbm, sharp_hbm, qkv_hbm, ex_ref, up_ref, dn_ref,
    w_ref, mix_ref, xo_ref, upg_ref, dng_ref,
    x_all, rows_buf, ent_buf, ext_buf, feats_buf, raw_buf, entt_buf, exg_ref, local_mat, all_mat, num_buf, mass_buf,
    piece_out, piece_in, qkv_ref, big_qkv, tok_buf, part_ref, sharp_ref,
    x_sem, own_sem, zs_sem, zr_sem, fs_sem, fr_sem, cs_sem, cr_sem,
    a_send, a_recv, t_send, t_recv,
):
    pts, wid, share, step, tile, head, slices, heads = sizes
    p, w = lax.axis_index("pts"), lax.axis_index("wid")
    total_rows, model = x_all.shape
    rows = rows_buf.shape[0]
    steps = total_rows // step
    tiles = rows // tile
    chips = share // 2
    group, core = p // share, p % 2
    chip = (p % share) // 2
    member = core * chips + chip
    mine_heads = heads // wid
    local_lanes = mine_heads * head
    local_wide = mine_heads * slices
    held = all_mat.shape[1] // head
    wide = held * slices
    groups = heads // held
    chunk = ex_ref.shape[0]

    def x_copy(t):
        at = pl.ds(pl.multiple_of(t * step, step), step)
        return pltpu.make_async_copy(x_ref.at[at], x_all.at[at], x_sem.at[t])

    small_copies = [
        pltpu.make_async_copy(ent_ref, ent_buf.at[w], own_sem.at[0]),
        pltpu.make_async_copy(part_hbm, part_ref, own_sem.at[1]),
        pltpu.make_async_copy(sharp_hbm, sharp_ref, own_sem.at[2]),
        pltpu.make_async_copy(qkv_hbm, qkv_ref, own_sem.at[3]),
    ]
    for copy in small_copies[:1]:
        copy.start()
    x_copy(0).start()
    for copy in small_copies[1:3]:
        copy.start()
    own_copies = []
    for m in range(1, 4):
        full = (exg_ref, upg_ref, dng_ref)[m - 1]
        own_copies.append(pltpu.make_async_copy(
            (ex_ref, up_ref, dn_ref)[m - 1],
            full.at[pl.ds(pl.multiple_of(w * chunk, chunk), chunk)], own_sem.at[m + 3],
        ))
    own_rows = pltpu.make_async_copy(
        x_ref.at[pl.ds(pl.multiple_of(w * rows, rows), rows)], xo_ref, own_sem.at[7]
    )

    barrier = pltpu.get_barrier_semaphore()
    for d in range(1, wid):
        pl.semaphore_signal(
            barrier, inc=1, device_id=(p, lax.rem(w + d, wid)), device_id_type=MESH
        )
    for d in range(1, pts):
        pl.semaphore_signal(
            barrier, inc=1, device_id=(lax.rem(p + d, pts), w), device_id_type=MESH
        )

    ent_part = ent_ref.shape[0] // share
    out_part = chunk // share

    def spot(m, owner, part, parts=1):
        if m == 0:
            count = ent_part * parts
            return ent_buf.at[owner, pl.ds(pl.multiple_of(part * count, count), count)]
        count = out_part * parts
        full = (exg_ref, upg_ref, dng_ref)[m - 1]
        return full.at[pl.ds(pl.multiple_of(owner * chunk + part * count, count), count)]

    def across(m, d):
        return pltpu.make_async_remote_copy(
            src_ref=spot(m, w, member), dst_ref=spot(m, w, member),
            send_sem=zs_sem.at[m, d - 1], recv_sem=zr_sem.at[m, d - 1],
            device_id=(p, lax.rem(w + d, wid)), device_id_type=MESH,
        )

    def forward(m, d, e):
        owner = lax.rem(w - d + wid, wid)
        to = group * share + 2 * lax.rem(chip + e, chips) + core
        return pltpu.make_async_remote_copy(
            src_ref=spot(m, owner, member), dst_ref=spot(m, owner, member),
            send_sem=fs_sem.at[m, d - 1, e - 1], recv_sem=fr_sem.at[m, d - 1, e - 1],
            device_id=(to, w), device_id_type=MESH,
        )

    def swap(m, d):
        owner = lax.rem(w - d + wid, wid)
        half = spot(m, owner, core, chips)
        return pltpu.make_async_remote_copy(
            src_ref=half, dst_ref=half,
            send_sem=cs_sem.at[m, d - 1], recv_sem=cr_sem.at[m, d - 1],
            device_id=(p + 1 - 2 * core, w), device_id_type=MESH,
        )

    def cross_all():
        for m in range(4):
            for d in range(1, wid):
                across(m, d).start()

    def pass_on(m):
        for d in range(1, wid):
            across(m, d).wait_recv()
            for e in range(1, chips):
                forward(m, d, e).start()

    def trade(m):
        for d in range(1, wid):
            for e in range(1, chips):
                forward(m, d, e).wait_recv()
            swap(m, d).start()

    def traded(m):
        for d in range(1, wid):
            swap(m, d).wait_recv()

    with jax.named_scope("setup"):
        ext_buf[:, :128] = jnp.zeros((model, 128), BF16)
        ext_buf[:, 128:] = jnp.full((model, 128), 1.0 / model, BF16)
        piece_out[...] = jnp.zeros_like(piece_out)
        num_buf[...] = jnp.zeros_like(num_buf)
        mass_buf[...] = jnp.zeros_like(mass_buf)
        local_mat[...] = jnp.zeros_like(local_mat)
        small_copies[0].wait()
        ext_buf[:, :local_lanes] = ent_buf[w]
        column_sum = jnp.sum(ext_buf[:, :128].astype(F32), axis=0, keepdims=True)
        x_copy(1).start()
        for copy in own_copies:
            copy.start()
        for t in range(2, min(4, steps)):
            x_copy(t).start()

    def tile_at(t):
        return pl.ds(pl.multiple_of(t * step, step), step)

    def project(t):
        return jnp.dot(x_all[tile_at(t), :], ext_buf[...], preferred_element_type=F32)

    def normalise(t, raw):
        narrow = x_all[tile_at(t), :]
        mean = raw[:, 128:]
        near = mean.astype(BF16)
        shift = mean - near.astype(F32)
        centred = narrow - jnp.concatenate([near] * (model // 128), axis=1)
        square = centred * centred
        while square.shape[1] > 128:
            half = square.shape[1] // 2
            square = square[:, :half] + square[:, half:]
        second = jnp.sum(square.astype(F32), axis=1, keepdims=True) * (1.0 / model)
        scale = lax.rsqrt(second - shift * shift + 1e-05)
        return ((raw[:, :128] - mean * column_sum) * scale).astype(BF16)

    def logits_of(feats):
        return lax.dot_general(local_mat[...].astype(BF16), feats, BOTH, preferred_element_type=F32)

    def collect(block, feats):
        num_buf[...] += jnp.dot(block, feats, preferred_element_type=F32)
        rounded = block.astype(F32)
        mass = rounded[:, :128]
        for c in range(1, block.shape[1] // 128):
            mass = mass + rounded[:, c * 128:(c + 1) * 128]
        mass_buf[...] += mass

    middle = (step // 128 + 1) // 2 * 128
    cuts = [slice(0, middle)] + ([slice(middle, step)] if middle < step else [])

    def ready(t):
        with jax.named_scope("xwait"):
            x_copy(t).wait()

    def fetch(t):
        if isinstance(t, int):
            if t < steps:
                x_copy(t).start()
        else:
            @pl.when(t < steps)
            def _():
                x_copy(t).start()

    def stage(t, slot, ahead):
        other = 1 - slot
        if ahead > 0:
            feats_buf[other] = normalise(t + 1, raw_buf[other])
        parts = [feats_buf[slot, c] for c in cuts]
        logits = [logits_of(part) for part in parts]
        if ahead > 1:
            raw_buf[slot] = project(t + 2)
        for one, part in zip(logits, parts):
            collect(slice_softmax(one, mine_heads, slices), part)

    pairs = (steps - 2) // 2

    def pair_step(i, carry):
        @pl.when(i == 0)
        def _():
            with jax.named_scope("barrier"):
                pl.semaphore_wait(barrier, wid - 1 + pts - 1)
                for copy in own_copies:
                    copy.wait()
                cross_all()

        @pl.when(i == pairs - 1)
        def _():
            with jax.named_scope("pass0"):
                pass_on(0)

        ready(2 * i + 2)
        ready(2 * i + 3)
        fetch(2 * i + 4)
        fetch(2 * i + 5)
        stage(2 * i, 0, 2)
        stage(2 * i + 1, 1, 2)
        return carry

    with jax.named_scope("numer"):
        x_copy(0).wait()
        raw_buf[0] = project(0)
        for copy in small_copies[1:3]:
            copy.wait()
        fill_logit_mat(local_mat, part_ref[...], sharp_ref[...], mine_heads, slices, head)
        x_copy(1).wait()
        feats_buf[0] = normalise(0, raw_buf[0])
        raw_buf[1] = project(1)
        lax.fori_loop(0, pairs, pair_step, 0)
        own_rows.start()
        small_copies[3].start()
        with jax.named_scope("pass1"):
            pass_on(1)
        for t in range(2 * pairs + 2, steps):
            ready(t)
        for t in range(2 * pairs, steps):
            stage(t, t % 2, min(2, steps - 1 - t))
    with jax.named_scope("pack"):
        lane = lax.broadcasted_iota(jnp.int32, (slices, 128), 1)
        packed = jnp.zeros((slices, 128), F32)
        for h in range(mine_heads):
            packed = jnp.where(lane // head == h, num_buf[pl.ds(h, slices, stride=mine_heads), :], packed)
        piece_out[:slices, :] = packed
        piece_out[slices:, :local_wide] = lax.dot_general(
            jnp.ones((8, 128), F32), mass_buf[...], BOTH, precision=HIGH, preferred_element_type=F32
        )
        spread = []
        for d in range(1, pts):
            spread.append(pltpu.make_async_remote_copy(
                src_ref=piece_out, dst_ref=piece_in.at[d - 1],
                send_sem=a_send.at[d - 1], recv_sem=a_recv.at[d - 1],
                device_id=(lax.rem(p + d, pts), w), device_id_type=MESH,
            ))
        for copy in spread:
            copy.start()
    with jax.named_scope("pass23"):
        trade(0)
        for m in range(2, 4):
            pass_on(m)
    with jax.named_scope("fill"):
        all_mat[...] = jnp.zeros_like(all_mat)
        big_qkv[...] = jnp.zeros_like(big_qkv)
        fill_logit_mat(all_mat, part_ref[...], sharp_ref[...], held, slices, head)
        small_copies[3].wait()
        for i in range(3):
            for h in range(mine_heads):
                at = slice(h * head, (h + 1) * head)
                big_qkv[i, at, at] = qkv_ref[i]
    own_rows.wait()
    norm_tile = pick_tile(rows, (704, 256, 128))

    def norm_step(t, carry):
        at = pl.ds(pl.multiple_of(t * norm_tile, norm_tile), norm_tile)
        rows_buf[at, :] = layer_norm(xo_ref[at, :].astype(F32)).astype(BF16)
        return carry

    with jax.named_scope("norm"):
        lax.fori_loop(0, rows // norm_tile, norm_step, 0)
    with jax.named_scope("traded0"):
        traded(0)
        trade(1)
    with jax.named_scope("entt"):
        width = ent_ref.shape[1]
        for owner in range(wid):
            entt_buf[owner * width:(owner + 1) * width, :] = ent_buf[owner].T

    def slice_step(t, carry):
        at = pl.ds(pl.multiple_of(t * tile, tile), tile)
        feats = lax.dot_general(
            entt_buf[...], rows_buf[at, :], BOTH, preferred_element_type=F32
        ).astype(BF16)
        lhs = all_mat[...].astype(BF16)
        for gi in range(groups):
            own = feats[gi * held * head:(gi + 1) * held * head]
            logits = jnp.dot(lhs, own, preferred_element_type=F32)
            w_ref[at, gi * wide:(gi + 1) * wide] = slice_softmax(logits, held, slices).T
        return carry

    with jax.named_scope("slice"):
        lax.fori_loop(0, tiles // 2, slice_step, 0)
    with jax.named_scope("sumwait"):
        total = piece_out[...]
        for d in range(1, pts):
            spread[d - 1].wait_recv()
            total = total + piece_in[d - 1]
    with jax.named_scope("token"):
        row = lax.broadcasted_iota(jnp.int32, (slices, local_wide), 0)
        col = lax.broadcasted_iota(jnp.int32, (slices, local_wide), 1)
        masses = jnp.ones((slices, 128), F32)
        for h in range(mine_heads):
            one = jnp.sum(
                jnp.where(col == row * mine_heads + h, total[slices:slices + 1, :local_wide], 0.0),
                axis=1, keepdims=True,
            )
            masses = jnp.where(lane // head == h, one, masses)
        tokens = total[:slices] / (masses + 1e-05)
        queries, keys_all, value_rows = (
            jnp.dot(tokens, big_qkv[i], precision=HIGH, preferred_element_type=F32) for i in range(3)
        )
        stacked = lambda a: jnp.concatenate(
            [jnp.where(lane // head == h, a, 0.0) for h in range(mine_heads)], axis=0
        )
        scores = lax.dot_general(
            queries, stacked(keys_all), BOTH, precision=HIGH, preferred_element_type=F32
        ) * (1.0 / head ** 0.5)
        owner_head = col // slices
        attend = jnp.zeros_like(scores)
        for h in range(mine_heads):
            part = jnp.where(owner_head == h, scores, -jnp.inf)
            power = jnp.exp(part - jnp.max(part, axis=1, keepdims=True))
            attend = attend + power / jnp.sum(power, axis=1, keepdims=True)
        tok_buf[w] = jnp.dot(
            attend, stacked(value_rows), precision=HIGH, preferred_element_type=F32
        ).astype(BF16)
        ring = []
        for d in range(1, wid):
            ring.append(pltpu.make_async_remote_copy(
                src_ref=tok_buf.at[w], dst_ref=tok_buf.at[w],
                send_sem=t_send.at[d - 1], recv_sem=t_recv.at[d - 1],
                device_id=(p, lax.rem(w + d, wid)), device_id_type=MESH,
            ))
        for copy in ring:
            copy.start()
    with jax.named_scope("slice"):
        lax.fori_loop(tiles // 2, tiles, slice_step, 0)
    with jax.named_scope("ringwait"):
        for m in range(2, 4):
            trade(m)
        traded(1)
        for copy in ring:
            copy.wait_recv()
    with jax.named_scope("mix"):
        row = lax.broadcasted_iota(jnp.int32, (wide, slices), 0) // held
        col = lax.broadcasted_iota(jnp.int32, (wide, slices), 1)
        repeat = jnp.where(row == col, 1.0, 0.0).astype(BF16)
        row = lax.broadcasted_iota(jnp.int32, (wide, held * head), 0) % held
        col = lax.broadcasted_iota(jnp.int32, (wide, held * head), 1) // head
        every = jnp.concatenate(
            [tok_buf[z].astype(F32)[:, :local_lanes] for z in range(wid)], axis=1
        ).astype(BF16)
        for gi in range(groups):
            lanes = slice(gi * held * head, (gi + 1) * held * head)
            block = jnp.dot(repeat, every[:, lanes], preferred_element_type=F32)
            block = jnp.where(row == col, block, 0.0).astype(BF16)
            mix_ref[gi * wide:(gi + 1) * wide, :] = jnp.dot(
                block, exg_ref[lanes, :], preferred_element_type=F32
            ).astype(BF16)
    with jax.named_scope("drain"):
        for m in range(2, 4):
            traded(m)
        for m in range(4):
            for d in range(1, wid):
                across(m, d).wait_send()
                swap(m, d).wait_send()
                for e in range(1, chips):
                    forward(m, d, e).wait_send()
        for copy in spread + ring:
            copy.wait_send()


def rows_kernel(
    step, w_ref, mix_ref, x_ref, upg_ref, dng_ref, out_ref,
    mid_buf, normed_buf, out_buf, out_sem,
):
    steps = x_ref.shape[0] // step
    model = x_ref.shape[1]

    def tile_at(t):
        return pl.ds(pl.multiple_of(t * step, step), step)

    def out_copy(t):
        return pltpu.make_async_copy(out_buf.at[t], out_ref.at[tile_at(t)], out_sem.at[t])

    def mix(t, slot):
        at = tile_at(t)
        midway = x_ref[at, :].astype(F32) + jnp.dot(
            w_ref[at, :], mix_ref[...], preferred_element_type=F32
        )
        mid_buf[slot] = midway
        centred = (midway - jnp.mean(midway, axis=1, keepdims=True)).astype(BF16)
        square = centred * centred
        while square.shape[1] > 128:
            half = square.shape[1] // 2
            square = square[:, :half] + square[:, half:]
        variance = jnp.sum(square.astype(F32), axis=1, keepdims=True) * (1.0 / model)
        scale = lax.rsqrt(variance + 1e-05).astype(BF16)
        normed_buf[slot] = centred * scale

    def feed(t, slot):
        before = jnp.dot(
            normed_buf[slot], upg_ref[...], preferred_element_type=F32
        ).astype(BF16)
        inner = before * (GELU_A + GELU_B * (before * before))
        half = 0.5 * before
        hidden = half + half * jnp.tanh(inner)
        out_buf[t] = (
            mid_buf[slot] + jnp.dot(hidden, dng_ref[...], preferred_element_type=F32)
        ).astype(BF16)

    with jax.named_scope("first"):
        mix(0, 0)
    for t in range(steps):
        with jax.named_scope("tail"):
            slot = t % 2
            if t + 1 < steps:
                mix(t + 1, 1 - slot)
            feed(t, slot)
            out_copy(t).start()
    with jax.named_scope("outwait"):
        for t in range(steps):
            out_copy(t).wait()


def local(x, entry, partition, sharpness, qkv, exit_m, widening, narrowing):
    pts, wid = lax.axis_size("pts"), lax.axis_size("wid")
    width = x.shape[1]
    head, slices = partition.shape
    heads = entry.shape[1] * wid // head
    mine = heads // wid
    rows = x.shape[0] // wid
    chunk = exit_m.shape[0]
    cells = heads * slices
    step = pick_tile(x.shape[0], (1024, 512, 256, 128))
    tile = pick_tile(rows, (1408, 256, 128))
    held = 256 // head
    share = 2
    for choice in (8, 4):
        if pts % choice == 0 and chunk % (16 * choice) == 0:
            share = choice
            break
    sizes = (pts, wid, share, step, tile, head, slices, heads)
    vmem = pl.BlockSpec(memory_space=pltpu.VMEM)
    hbm = pl.BlockSpec(memory_space=pltpu.HBM)
    dma = pltpu.SemaphoreType.DMA
    full = pltpu.VMEM((chunk * wid, width), BF16)
    hops = max(share // 2 - 1, 1)
    pin = lambda a: pltpu.with_memory_space_constraint(a, pltpu.HBM)
    weights, mix, own, upg, dng = pl.pallas_call(
        functools.partial(gather_kernel, sizes),
        name="slices_and_gather",
        out_shape=(
            pltpu.VMEM((rows, cells), BF16),
            pltpu.VMEM((cells, width), BF16),
            pltpu.VMEM((rows, width), BF16),
            full, full,
        ),
        in_specs=[hbm] * 8,
        out_specs=(vmem,) * 5,
        scratch_shapes=[
            pltpu.VMEM(x.shape, BF16),
            pltpu.VMEM((rows, width), BF16),
            pltpu.VMEM((wid,) + entry.shape, BF16),
            pltpu.VMEM((width, 256), BF16),
            pltpu.VMEM((2, step, 128), BF16),
            pltpu.VMEM((2, step, 256), F32),
            pltpu.VMEM((entry.shape[1] * wid, entry.shape[0]), BF16),
            pltpu.VMEM((chunk * wid, width), BF16),
            pltpu.VMEM((mine * slices + 16, 128), F32),
            pltpu.VMEM((held * slices + 16, held * head), F32),
            pltpu.VMEM((mine * slices, 128), F32),
            pltpu.VMEM((mine * slices, 128), F32),
            pltpu.VMEM((slices + 8, 128), F32),
            pltpu.VMEM((pts - 1, slices + 8, 128), F32),
            pltpu.VMEM(qkv.shape, F32),
            pltpu.VMEM((3, 128, 128), F32),
            pltpu.VMEM((wid, slices, 128), BF16),
            pltpu.VMEM((slices, head), BF16),
            pltpu.VMEM((1, head), F32),
            dma((x.shape[0] // step,)), dma((8,)),
            dma((4, wid - 1)), dma((4, wid - 1)),
            dma((4, wid - 1, hops)), dma((4, wid - 1, hops)),
            dma((4, wid - 1)), dma((4, wid - 1)),
            dma((pts - 1,)), dma((pts - 1,)),
            dma((wid - 1,)), dma((wid - 1,)),
        ],
        compiler_params=pltpu.CompilerParams(
            collective_id=0, has_side_effects=True, vmem_limit_bytes=44 * 1024 * 1024
        ),
    )(
        pin(x), pin(entry), pin(partition.T), pin(sharpness.reshape(1, head)), pin(qkv),
        pin(exit_m), pin(widening), pin(narrowing),
    )

    step = pick_tile(rows, (704, 256, 128))
    return pl.pallas_call(
        functools.partial(rows_kernel, step),
        name="mix_and_feed",
        out_shape=jax.ShapeDtypeStruct((rows, width), BF16),
        in_specs=[vmem] * 5,
        out_specs=pl.BlockSpec(memory_space=pl.ANY),
        scratch_shapes=[
            pltpu.VMEM((2, step, width), F32),
            pltpu.VMEM((2, step, width), BF16),
            pltpu.VMEM((rows // step, step, width), BF16),
            dma((rows // step,)),
        ],
        compiler_params=pltpu.CompilerParams(vmem_limit_bytes=40 * 1024 * 1024),
    )(weights, mix, own, upg, dng)


def solution(mesh):
    placed = (
        P("pts", None),
        P(None, "wid"),
        P(),
        P(),
        P(),
        P("wid", None),
        P("wid", None),
        P("wid", None),
    )
    return jax.shard_map(
        local, mesh=mesh, in_specs=placed, out_specs=P(("pts", "wid"), None), check_vma=False
    )
```

time: 43.6 us -> 31.9 us (0.73)
  local copies, waits for them, and re-layouts: 5.86 us -> 0 us
  Pallas kernels: 37.5 us -> 31.7 us
    unnamed x14 -> x0, local copies, waits for them, and re-layouts: 5.86 us -> none
    pallas_call x1, Pallas kernels: 29.6 us -> 26.5 us  [local(): pl.pallas_call(functools.partial(gather_kernel, sizes), name='slices_and_...]
    pallas_call x1, Pallas kernels: 7.83 us -> 5.21 us  [local(): pl.pallas_call(functools.partial(rows_kernel, step), name='mix_and_feed',...]
where the time goes in v2:
time: 31.9 us; the launch traced here: 31.7 us
  Pallas kernels  31.7 us (99%)
    pallas_call x1, Pallas kernels, local(): pl.pallas_call(functools.partial(gather_kernel, sizes), name='slices_and_...  26.5 us
    pallas_call x1, Pallas kernels, local(): pl.pallas_call(functools.partial(rows_kernel, step), name='mix_and_feed',...  5.21 us

profile of v2, /device:TPU:0, one launch (start us, length us, event | category | flops | bytes accessed | tf_op | source)
XLA Modules:
  0.0 31.7 jit_solution(17079916304710658199)
XLA Ops:
  0.0 26.5 %slices_and_gather.1 = (bf16[2816,256]{1,0:T(8,128)(2,1)S(1)}, bf16[256,512]{1,0:T(8,128)(2,1)S(1)}, bf16[2816,512]{1,0:T(8,128)(2,1)S(1)}, bf16[512,512]{1,0:T(8,128)(2,1)S(1)}, bf16[512,512]{1,0:T(8,128)(2,1)S(1)}) custom-call(bf16[11264,512]{1,0:T(8,128)(2,1)} %x_ref.1, bf16[512,128]{1,0:T(8,128)(2,1)} %ent_ref.1, bf16[32,64]{1,0:T(8,128)(2,1)} %bitcast.2, ...), custom_call_target="tpu_custom_call" | custom-call | tf_op jit(solution)/shard_map/slices_and_gather/pallas_call | solution.py:527
  26.5 5.2 %mix_and_feed.1 = bf16[2816,512]{1,0:T(8,128)(2,1)} custom-call(bf16[2816,256]{1,0:T(8,128)(2,1)S(1)} %get-tuple-element.10.w_ref, bf16[256,512]{1,0:T(8,128)(2,1)S(1)} %get-tuple-element.11.mix_ref, bf16[2816,512]{1,0:T(8,128)(2,1)S(1)} %get-tuple-element.12.x_ref, bf16[512,512]{1,0:T(8,128)(2,1)S(1)} %get-tuple-element.13.upg_ref, ...), custom_call_target="tpu_custom_call" | custom-call | tf_op jit(solution)/shard_map/mix_and_feed/pallas_call | solution.py:574

commit v3 on v2

v3 whole, which is shorter than its diff:
```python
import functools
import math

import jax
import jax.numpy as jnp
from jax import lax
from jax.experimental import pallas as pl
from jax.experimental.pallas import tpu as pltpu
from jax.sharding import PartitionSpec as P

MESH = pl.DeviceIdType.MESH
F32 = jnp.float32
BF16 = jnp.bfloat16
HIGH = lax.Precision.HIGHEST
LOG2E = math.log2(math.e)
BOTH = (((1,), (1,)), ((), ()))
GELU_A = math.sqrt(2.0 / math.pi)
GELU_B = 0.044715 * math.sqrt(2.0 / math.pi)


def layer_norm(values):
    centred = values - jnp.mean(values, axis=-1, keepdims=True)
    variance = jnp.mean(centred * centred, axis=-1, keepdims=True)
    return centred * lax.rsqrt(variance + 1e-05)


def pick_tile(rows, choices):
    for choice in choices:
        if rows % choice == 0:
            return choice
    return rows


def fold_rows(values, held, combine):
    shift = 4
    while shift >= held:
        values = combine(values, pltpu.roll(values, shift, 0))
        shift //= 2
    return values


def point_stats(stat, wide, model):
    mean = stat[wide + 16:wide + 24]
    shift = mean - mean.astype(BF16).astype(F32)
    variance = stat[wide + 24:wide + 32] * (1.0 / model) - shift * shift
    return mean, lax.rsqrt(variance + 1e-05)


def slice_softmax(stat, sums, mean, scale, held, slices):
    wide = held * slices
    points = stat.shape[1]
    across_points = lambda a: jnp.concatenate([a] * (points // 128), axis=1)
    raw = stat[wide:wide + 8] + stat[wide + 8:wide + 16]
    raw = (raw - mean * across_points(sums[wide:wide + 8] + sums[wide + 8:wide + 16])) * scale
    soft = jnp.maximum(raw, 0.0) + jnp.log1p(jnp.exp(-jnp.abs(raw)))
    inverse = LOG2E / (0.5 + soft) * scale
    shape = (wide // 8, 8, points)
    offset = across_points(sums[:wide]).reshape(shape) * mean[None]
    score = (stat[:wide].reshape(shape) - offset) * inverse[None]
    top = fold_rows(jnp.max(score, axis=0), held, jnp.maximum)
    power = jnp.exp2(score - top[None])
    return power, 1.0 / fold_rows(jnp.sum(power, axis=0), held, jnp.add)


def fill_logit_mat(mat, part_t, sharp, held, slices, head):
    wide = held * slices
    sharp_hi = sharp.astype(BF16).astype(F32)
    sharp_lo = sharp - sharp_hi
    small = lax.broadcasted_iota(jnp.int32, (8, head), 0) % held
    part = jnp.concatenate([part_t.astype(F32)] * (128 // head), axis=1)
    lane = lax.broadcasted_iota(jnp.int32, part.shape, 1)
    for h in range(held):
        lanes = slice(h * head, (h + 1) * head)
        mat[pl.ds(h, slices, stride=held), :] = jnp.where(lane // head == h, part, 0.0)
        mat[wide:wide + 8, lanes] = jnp.where(small == h, sharp_hi, 0.0)
        mat[wide + 8:wide + 16, lanes] = jnp.where(small == h, sharp_lo, 0.0)


def gather_kernel(
    sizes, x_ref, ent_ref, part_hbm, sharp_hbm, qkv_hbm, ex_ref, up_ref, dn_ref,
    w_ref, mix_ref, xo_ref, upg_ref, dng_ref,
    x_all, ent_buf, ep_buf, ext_buf, feats_buf, raw_buf, stat_buf, sums_buf, mean_all, scale_all,
    lhs_buf, lhs_sums, exg_ref, local_mat, num_buf, mass_buf,
    piece_out, piece_in, qkv_ref, big_qkv, tok_buf, part_ref, sharp_ref,
    x_sem, own_sem, zs_sem, zr_sem, fs_sem, fr_sem, cs_sem, cr_sem,
    a_send, a_recv, t_send, t_recv,
):
    pts, wid, share, step, tile, head, slices, heads = sizes
    p, w = lax.axis_index("pts"), lax.axis_index("wid")
    total_rows, model = x_all.shape
    rows = xo_ref.shape[0]
    steps = total_rows // step
    tiles = rows // tile
    chips = share // 2
    group, core = p // share, p % 2
    chip = (p % share) // 2
    member = core * chips + chip
    mine_heads = heads // wid
    local_lanes = mine_heads * head
    local_wide = mine_heads * slices
    fold = local_wide + 16
    chunk = ex_ref.shape[0]

    def x_copy(t):
        at = pl.ds(pl.multiple_of(t * step, step), step)
        return pltpu.make_async_copy(x_ref.at[at], x_all.at[at], x_sem.at[t])

    small_copies = [
        pltpu.make_async_copy(ent_ref, ent_buf, own_sem.at[0]),
        pltpu.make_async_copy(part_hbm, part_ref, own_sem.at[1]),
        pltpu.make_async_copy(sharp_hbm, sharp_ref, own_sem.at[2]),
        pltpu.make_async_copy(qkv_hbm, qkv_ref, own_sem.at[3]),
    ]
    for copy in small_copies[:1]:
        copy.start()
    for copy in small_copies[1:3]:
        copy.start()
    for t in range(min(2, steps)):
        x_copy(t).start()
    own_copies = []
    for m in range(1, 4):
        full = (exg_ref, upg_ref, dng_ref)[m - 1]
        own_copies.append(pltpu.make_async_copy(
            (ex_ref, up_ref, dn_ref)[m - 1],
            full.at[pl.ds(pl.multiple_of(w * chunk, chunk), chunk)], own_sem.at[m + 3],
        ))
    own_rows = pltpu.make_async_copy(
        x_ref.at[pl.ds(pl.multiple_of(w * rows, rows), rows)], xo_ref, own_sem.at[7]
    )

    barrier = pltpu.get_barrier_semaphore()
    for d in range(1, wid):
        pl.semaphore_signal(
            barrier, inc=1, device_id=(p, lax.rem(w + d, wid)), device_id_type=MESH
        )
    for d in range(1, pts):
        pl.semaphore_signal(
            barrier, inc=1, device_id=(lax.rem(p + d, pts), w), device_id_type=MESH
        )

    out_part = chunk // share
    paired = {2: 1, 3: 2} if chips == 4 else {}
    blocks_each = ep_buf.shape[1] // chips

    def spot(m, owner, whole=False):
        if m == 0:
            at = pl.ds(pl.multiple_of(core * (fold // 2), 8), fold // 2)
            if whole:
                return ep_buf.at[owner, :, at]
            return ep_buf.at[owner, pl.ds(chip * blocks_each, blocks_each), at]
        full = (exg_ref, upg_ref, dng_ref)[m - 1]
        if whole:
            part, count = core, chunk // 2
        elif m in paired:
            part, count = core * 2 + chip // paired[m] % 2, chunk // 4
        else:
            part, count = member, out_part
        return full.at[pl.ds(pl.multiple_of(owner * chunk + part * count, count), count)]

    def hops(m):
        return 1 if m in paired else chips - 1

    def across(m, d):
        return pltpu.make_async_remote_copy(
            src_ref=spot(m, w), dst_ref=spot(m, w),
            send_sem=zs_sem.at[m, d - 1], recv_sem=zr_sem.at[m, d - 1],
            device_id=(p, lax.rem(w + d, wid)), device_id_type=MESH,
        )

    def forward(m, d, e):
        owner = lax.rem(w - d + wid, wid)
        if m in paired:
            other = chip + paired[m] * (1 - 2 * (chip // paired[m] % 2))
        else:
            other = lax.rem(chip + e, chips)
        to = group * share + 2 * other + core
        return pltpu.make_async_remote_copy(
            src_ref=spot(m, owner), dst_ref=spot(m, owner),
            send_sem=fs_sem.at[m, d - 1, e - 1], recv_sem=fr_sem.at[m, d - 1, e - 1],
            device_id=(to, w), device_id_type=MESH,
        )

    def swap(m, d):
        owner = lax.rem(w - d + wid, wid)
        half = spot(m, owner, True)
        return pltpu.make_async_remote_copy(
            src_ref=half, dst_ref=half,
            send_sem=cs_sem.at[m, d - 1], recv_sem=cr_sem.at[m, d - 1],
            device_id=(p + 1 - 2 * core, w), device_id_type=MESH,
        )

    def cross_all():
        for m in range(4):
            for d in range(1, wid):
                across(m, d).start()

    def pass_on(m):
        for d in range(1, wid):
            across(m, d).wait_recv()
            for e in range(1, hops(m) + 1):
                forward(m, d, e).start()

    def trade(m):
        for d in range(1, wid):
            for e in range(1, hops(m) + 1):
                forward(m, d, e).wait_recv()
            swap(m, d).start()

    def traded(m):
        for d in range(1, wid):
            swap(m, d).wait_recv()

    with jax.named_scope("setup"):
        ext_buf[:, :128] = jnp.zeros((model, 128), BF16)
        piece_out[...] = jnp.zeros_like(piece_out)
        num_buf[...] = jnp.zeros_like(num_buf)
        mass_buf[...] = jnp.zeros_like(mass_buf)
        local_mat[...] = jnp.zeros_like(local_mat)
        for copy in small_copies[1:3]:
            copy.wait()
        for t in range(2, min(4, steps)):
            x_copy(t).start()
        for copy in own_copies:
            copy.start()
        fill_logit_mat(local_mat, part_ref[...], sharp_ref[...], mine_heads, slices, head)
        small_copies[0].wait()
        ext_buf[:, :local_lanes] = ent_buf[...]
        own = ext_buf[:, :128]
        column_sum = jnp.sum(own.astype(F32), axis=0, keepdims=True)
        main, fine = local_mat[...], local_mat[local_wide + 8:local_wide + 16]
        coarse = main[local_wide:local_wide + 8]
        blank = jnp.zeros((128 - local_wide - 16, 128), F32)
        first = jnp.concatenate([main[:local_wide], coarse, coarse, blank], axis=0)
        second = jnp.concatenate([jnp.zeros((local_wide, 128), F32), fine, fine, blank], axis=0)
        first, second = first.astype(BF16), second.astype(BF16)
        folded = lax.dot_general(own, first, BOTH, preferred_element_type=F32) + lax.dot_general(
            own, second, BOTH, preferred_element_type=F32
        )
        lanes = lax.broadcasted_iota(jnp.int32, folded.shape, 1)
        rounded = folded.astype(BF16).astype(F32)
        picked = jnp.where(
            jnp.logical_and(lanes >= local_wide + 8, lanes < local_wide + 16),
            folded - rounded, rounded,
        )
        picked = jnp.where(lanes >= local_wide + 16, 1.0 / model, picked)
        ext_buf[:, 128:] = picked.astype(BF16)

    def tile_at(t):
        return pl.ds(pl.multiple_of(t * step, step), step)

    def project(t):
        return jnp.dot(x_all[tile_at(t), :], ext_buf[...], preferred_element_type=F32)

    stat_lane = lax.broadcasted_iota(jnp.int32, (step, 128), 1)

    def prepare(t, slot):
        narrow = x_all[tile_at(t), :]
        rest = raw_buf[slot, :, 128:]
        mean = jnp.broadcast_to(rest[:, local_wide + 16:local_wide + 17], rest.shape)
        near = mean.astype(BF16)
        centred = narrow - jnp.concatenate([near] * (model // 128), axis=1)
        square = centred * centred
        while square.shape[1] > 128:
            half = square.shape[1] // 2
            square = square[:, :half] + square[:, half:]
        second = jnp.sum(square.astype(F32), axis=1, keepdims=True)
        feats_buf[slot] = (raw_buf[slot, :, :128] - mean * column_sum).astype(BF16)
        rest = jnp.where(stat_lane >= local_wide + 24, second, rest)
        stat_buf[slot] = rest.T[:local_wide + 32]

    def collect(t, slot):
        stat = stat_buf[slot]
        mean, scale = point_stats(stat, local_wide, model)
        mean_all[:, t * step:(t + 1) * step] = mean
        scale_all[:, t * step:(t + 1) * step] = scale
        power, total = slice_softmax(stat, sums_buf[...], mean, scale, mine_heads, slices)
        weights = (power * total[None]).reshape(local_wide, step)
        scaled = (power * (total * scale)[None]).reshape(local_wide, step).astype(BF16)
        num_buf[...] += jnp.dot(scaled, feats_buf[slot], preferred_element_type=F32)
        mass = weights[:, :128]
        for c in range(1, step // 128):
            mass = mass + weights[:, c * 128:(c + 1) * 128]
        mass_buf[...] += mass

    blocks = (steps + 1) // 2 + 2
    for b in range(blocks):
        if b == 1:
            with jax.named_scope("barrier"):
                pl.semaphore_wait(barrier, wid - 1 + pts - 1)
                for copy in own_copies:
                    copy.wait()
                cross_all()
                own_rows.start()
                small_copies[3].start()
        if b == blocks - 4:
            with jax.named_scope("pass0"):
                pass_on(0)
        with jax.named_scope("xwait"):
            for t in range(2 * b, min(2 * b + 2, steps)):
                x_copy(t).wait()
            for t in range(2 * b + 4, min(2 * b + 6, steps)):
                x_copy(t).start()
        with jax.named_scope("block"):
            for t in range(2 * b, min(2 * b + 2, steps)):
                raw_buf[t % 4] = project(t)
            if b == 0:
                folded = lax.dot_general(
                    first, own, BOTH, preferred_element_type=F32
                ) + lax.dot_general(second, own, BOTH, preferred_element_type=F32)
                row = lax.broadcasted_iota(jnp.int32, folded.shape, 0)
                rounded = folded.astype(BF16).astype(F32)
                picked = jnp.where(row >= local_wide + 8, folded - rounded, rounded)[:fold]
                for c in range(model // 128):
                    ep_buf[w, c] = picked[:, c * 128:(c + 1) * 128].astype(BF16)
                sums_buf[...] = lax.dot_general(
                    ext_buf[:, 128:], jnp.ones((model, 128), BF16), (((0,), (0,)), ((), ())),
                    preferred_element_type=F32,
                )
            for t in range(2 * b - 2, min(2 * b, steps)):
                if t >= 0:
                    prepare(t, t % 4)
            for t in range(2 * b - 4, min(2 * b - 2, steps)):
                if t >= 0:
                    collect(t, t % 4)
    with jax.named_scope("pack"):
        lane = lax.broadcasted_iota(jnp.int32, (slices, 128), 1)
        packed = jnp.zeros((slices, 128), F32)
        for h in range(mine_heads):
            packed = jnp.where(lane // head == h, num_buf[pl.ds(h, slices, stride=mine_heads), :], packed)
        masses = lax.dot_general(
            jnp.ones((8, 128), F32), mass_buf[...], BOTH, precision=HIGH,
            preferred_element_type=F32,
        )
        rounded = masses.astype(BF16).astype(F32)
        piece_out[:slices, :] = packed.astype(BF16)
        piece_out[slices:, :local_wide] = jnp.concatenate(
            [rounded, masses - rounded], axis=0
        ).astype(BF16)
        spread = []
        for d in range(1, pts):
            spread.append(pltpu.make_async_remote_copy(
                src_ref=piece_out, dst_ref=piece_in.at[d - 1],
                send_sem=a_send.at[d - 1], recv_sem=a_recv.at[d - 1],
                device_id=(lax.rem(p + d, pts), w), device_id_type=MESH,
            ))
        for copy in spread:
            copy.start()
    with jax.named_scope("pass1"):
        pass_on(1)
    with jax.named_scope("fill"):
        big_qkv[...] = jnp.zeros_like(big_qkv)
        small_copies[3].wait()
        for i in range(3):
            for h in range(mine_heads):
                at = slice(h * head, (h + 1) * head)
                big_qkv[i, at, at] = qkv_ref[i]
    with jax.named_scope("pass2"):
        pass_on(2)
    with jax.named_scope("pass3"):
        pass_on(3)
    with jax.named_scope("trade0"):
        trade(0)

    def slice_step(t, carry):
        at = pl.ds(pl.multiple_of(t * tile, tile), tile)
        there = pl.ds(pl.multiple_of(w * rows + t * tile, 128), tile)
        stat = lax.dot_general(lhs_buf[...], xo_ref[at, :], BOTH, preferred_element_type=F32)
        mean, scale = mean_all[:, there], scale_all[:, there]
        parts = []
        for owner in range(wid):
            mine = slice(owner * fold, (owner + 1) * fold)
            power, total = slice_softmax(
                stat[mine], lhs_sums[mine], mean, scale, mine_heads, slices
            )
            parts.append((power * total[None]).reshape(local_wide, tile).astype(BF16))
        w_ref[at, :] = jnp.concatenate(parts, axis=0).T
        return carry

    with jax.named_scope("sumwait"):
        total = piece_out[...].astype(F32)
        for d in range(1, pts):
            spread[d - 1].wait_recv()
            total = total + piece_in[d - 1].astype(F32)
        mass_row = total[slices:slices + 1] + total[slices + 8:slices + 9]
    with jax.named_scope("token"):
        row = lax.broadcasted_iota(jnp.int32, (slices, local_wide), 0)
        col = lax.broadcasted_iota(jnp.int32, (slices, local_wide), 1)
        masses = jnp.ones((slices, 128), F32)
        for h in range(mine_heads):
            one = jnp.sum(
                jnp.where(col == row * mine_heads + h, mass_row[:, :local_wide], 0.0),
                axis=1, keepdims=True,
            )
            masses = jnp.where(lane // head == h, one, masses)
        tokens = total[:slices] / (masses + 1e-05)
        queries, keys_all, value_rows = (
            jnp.dot(tokens, big_qkv[i], precision=HIGH, preferred_element_type=F32) for i in range(3)
        )
        stacked = lambda a: jnp.concatenate(
            [jnp.where(lane // head == h, a, 0.0) for h in range(mine_heads)], axis=0
        )
        scores = lax.dot_general(
            queries, stacked(keys_all), BOTH, precision=HIGH, preferred_element_type=F32
        ) * (1.0 / head ** 0.5)
        owner_head = col // slices
        attend = jnp.zeros_like(scores)
        for h in range(mine_heads):
            part = jnp.where(owner_head == h, scores, -jnp.inf)
            power = jnp.exp(part - jnp.max(part, axis=1, keepdims=True))
            attend = attend + power / jnp.sum(power, axis=1, keepdims=True)
        tok_buf[w] = jnp.dot(
            attend, stacked(value_rows), precision=HIGH, preferred_element_type=F32
        ).astype(BF16)
        ring = []
        for d in range(1, wid):
            ring.append(pltpu.make_async_remote_copy(
                src_ref=tok_buf.at[w], dst_ref=tok_buf.at[w],
                send_sem=t_send.at[d - 1], recv_sem=t_recv.at[d - 1],
                device_id=(p, lax.rem(w + d, wid)), device_id_type=MESH,
            ))
        for copy in ring:
            copy.start()
    with jax.named_scope("traded0"):
        traded(0)
        own_rows.wait()
    with jax.named_scope("entt"):
        for owner in range(wid):
            for c in range(model // 128):
                lhs_buf[owner * fold:(owner + 1) * fold, c * 128:(c + 1) * 128] = ep_buf[owner, c]
        lhs_sums[...] = jnp.dot(
            lhs_buf[...], jnp.ones((model, 128), BF16), preferred_element_type=F32
        )
    with jax.named_scope("slice"):
        lax.fori_loop(0, tiles // 2, slice_step, 0)
    with jax.named_scope("trade1"):
        trade(1)
    with jax.named_scope("slice"):
        lax.fori_loop(tiles // 2, tiles, slice_step, 0)
    with jax.named_scope("ringwait"):
        for m in range(2, 4):
            trade(m)
        traded(1)
        for copy in ring:
            copy.wait_recv()
    with jax.named_scope("mix"):
        row = lax.broadcasted_iota(jnp.int32, (local_wide, slices), 0) // mine_heads
        col = lax.broadcasted_iota(jnp.int32, (local_wide, slices), 1)
        repeat = jnp.where(row == col, 1.0, 0.0).astype(BF16)
        row = lax.broadcasted_iota(jnp.int32, (local_wide, 128), 0) % mine_heads
        col = lax.broadcasted_iota(jnp.int32, (local_wide, 128), 1) // head
        for z in range(wid):
            block = jnp.dot(repeat, tok_buf[z], preferred_element_type=F32)
            block = jnp.where(row == col, block, 0.0).astype(BF16)[:, :local_lanes]
            mix_ref[z * local_wide:(z + 1) * local_wide, :] = jnp.dot(
                block, exg_ref[z * local_lanes:(z + 1) * local_lanes, :],
                preferred_element_type=F32,
            ).astype(BF16)
    with jax.named_scope("drain"):
        for m in range(2, 4):
            traded(m)
        for m in range(4):
            for d in range(1, wid):
                across(m, d).wait_send()
                swap(m, d).wait_send()
                for e in range(1, hops(m) + 1):
                    forward(m, d, e).wait_send()
        for copy in spread + ring:
            copy.wait_send()


def rows_kernel(
    step, w_ref, mix_ref, x_ref, upg_ref, dng_ref, out_ref,
    mid_buf, normed_buf, out_buf, out_sem,
):
    steps = x_ref.shape[0] // step
    model = x_ref.shape[1]

    def tile_at(t):
        return pl.ds(pl.multiple_of(t * step, step), step)

    def out_copy(t):
        return pltpu.make_async_copy(out_buf.at[t], out_ref.at[tile_at(t)], out_sem.at[t])

    def mix(t, slot):
        at = tile_at(t)
        midway = x_ref[at, :].astype(F32) + jnp.dot(
            w_ref[at, :], mix_ref[...], preferred_element_type=F32
        )
        mid_buf[slot] = midway
        centred = (midway - jnp.mean(midway, axis=1, keepdims=True)).astype(BF16)
        square = centred * centred
        while square.shape[1] > 128:
            half = square.shape[1] // 2
            square = square[:, :half] + square[:, half:]
        variance = jnp.sum(square.astype(F32), axis=1, keepdims=True) * (1.0 / model)
        scale = lax.rsqrt(variance + 1e-05).astype(BF16)
        normed_buf[slot] = centred * scale

    def feed(t, slot):
        before = jnp.dot(
            normed_buf[slot], upg_ref[...], preferred_element_type=F32
        ).astype(BF16)
        inner = before * (GELU_A + GELU_B * (before * before))
        half = 0.5 * before
        hidden = half + half * jnp.tanh(inner)
        out_buf[t] = (
            mid_buf[slot] + jnp.dot(hidden, dng_ref[...], preferred_element_type=F32)
        ).astype(BF16)

    with jax.named_scope("first"):
        mix(0, 0)
    for t in range(steps):
        with jax.named_scope("tail"):
            slot = t % 2
            if t + 1 < steps:
                mix(t + 1, 1 - slot)
            feed(t, slot)
            out_copy(t).start()
    with jax.named_scope("outwait"):
        for t in range(steps):
            out_copy(t).wait()


def local(x, entry, partition, sharpness, qkv, exit_m, widening, narrowing):
    pts, wid = lax.axis_size("pts"), lax.axis_size("wid")
    width = x.shape[1]
    head, slices = partition.shape
    heads = entry.shape[1] * wid // head
    mine = heads // wid
    rows = x.shape[0] // wid
    chunk = exit_m.shape[0]
    cells = heads * slices
    step = pick_tile(x.shape[0], (1024, 512, 256, 128))
    tile = pick_tile(rows, (1408, 256, 128))
    fold = mine * slices + 16
    share = 2
    for choice in (8, 4):
        if pts % choice == 0 and chunk % (16 * choice) == 0:
            share = choice
            break
    sizes = (pts, wid, share, step, tile, head, slices, heads)
    vmem = pl.BlockSpec(memory_space=pltpu.VMEM)
    hbm = pl.BlockSpec(memory_space=pltpu.HBM)
    dma = pltpu.SemaphoreType.DMA
    full = pltpu.VMEM((chunk * wid, width), BF16)
    hops = max(share // 2 - 1, 1)
    pin = lambda a: pltpu.with_memory_space_constraint(a, pltpu.HBM)
    weights, mix, own, upg, dng = pl.pallas_call(
        functools.partial(gather_kernel, sizes),
        name="slices_and_gather",
        out_shape=(
            pltpu.VMEM((rows, cells), BF16),
            pltpu.VMEM((cells, width), BF16),
            pltpu.VMEM((rows, width), BF16),
            full, full,
        ),
        in_specs=[hbm] * 8,
        out_specs=(vmem,) * 5,
        scratch_shapes=[
            pltpu.VMEM(x.shape, BF16),
            pltpu.VMEM(entry.shape, BF16),
            pltpu.VMEM((wid, width // 128, fold, 128), BF16),
            pltpu.VMEM((width, 256), BF16),
            pltpu.VMEM((4, step, 128), BF16),
            pltpu.VMEM((4, step, 256), F32),
            pltpu.VMEM((4, mine * slices + 32, step), F32),
            pltpu.VMEM((128, 128), F32),
            pltpu.VMEM((8, x.shape[0]), F32),
            pltpu.VMEM((8, x.shape[0]), F32),
            pltpu.VMEM((wid * fold, width), BF16),
            pltpu.VMEM((wid * fold, 128), F32),
            pltpu.VMEM((chunk * wid, width), BF16),
            pltpu.VMEM((fold, 128), F32),
            pltpu.VMEM((mine * slices, 128), F32),
            pltpu.VMEM((mine * slices, 128), F32),
            pltpu.VMEM((slices + 16, 128), BF16),
            pltpu.VMEM((pts - 1, slices + 16, 128), BF16),
            pltpu.VMEM(qkv.shape, F32),
            pltpu.VMEM((3, 128, 128), F32),
            pltpu.VMEM((wid, slices, 128), BF16),
            pltpu.VMEM((slices, head), BF16),
            pltpu.VMEM((1, head), F32),
            dma((x.shape[0] // step,)), dma((8,)),
            dma((4, wid - 1)), dma((4, wid - 1)),
            dma((4, wid - 1, hops)), dma((4, wid - 1, hops)),
            dma((4, wid - 1)), dma((4, wid - 1)),
            dma((pts - 1,)), dma((pts - 1,)),
            dma((wid - 1,)), dma((wid - 1,)),
        ],
        compiler_params=pltpu.CompilerParams(
            collective_id=0, has_side_effects=True, vmem_limit_bytes=44 * 1024 * 1024
        ),
    )(
        pin(x), pin(entry), pin(partition.T), pin(sharpness.reshape(1, head)), pin(qkv),
        pin(exit_m), pin(widening), pin(narrowing),
    )

    step = pick_tile(rows, (704, 256, 128))
    return pl.pallas_call(
        functools.partial(rows_kernel, step),
        name="mix_and_feed",
        out_shape=jax.ShapeDtypeStruct((rows, width), BF16),
        in_specs=[vmem] * 5,
        out_specs=pl.BlockSpec(memory_space=pl.ANY),
        scratch_shapes=[
            pltpu.VMEM((2, step, width), F32),
            pltpu.VMEM((2, step, width), BF16),
            pltpu.VMEM((rows // step, step, width), BF16),
            dma((rows // step,)),
        ],
        compiler_params=pltpu.CompilerParams(vmem_limit_bytes=40 * 1024 * 1024),
    )(weights, mix, own, upg, dng)


def solution(mesh):
    placed = (
        P("pts", None),
        P(None, "wid"),
        P(),
        P(),
        P(),
        P("wid", None),
        P("wid", None),
        P("wid", None),
    )
    return jax.shard_map(
        local, mesh=mesh, in_specs=placed, out_specs=P(("pts", "wid"), None), check_vma=False
    )
```

time: 31.9 us -> 30.1 us (0.944)
  Pallas kernels: 31.7 us -> 29.8 us
    pallas_call x1, Pallas kernels: 26.5 us -> 24.4 us  [local(): pl.pallas_call(functools.partial(gather_kernel, sizes), name='slices_and_...]
where the time goes in v3:
time: 30.1 us; the launch traced here: 30 us
  Pallas kernels  29.8 us (99%)
    pallas_call x1, Pallas kernels, local(): pl.pallas_call(functools.partial(gather_kernel, sizes), name='slices_and_...  24.4 us
    pallas_call x1, Pallas kernels, local(): pl.pallas_call(functools.partial(rows_kernel, step), name='mix_and_feed',...  5.41 us

profile of v3, /device:TPU:0, one launch (start us, length us, event | category | flops | bytes accessed | tf_op | source)
XLA Modules:
  0.0 30.0 jit_solution(5088293295541997005)
XLA Ops:
  0.0 24.4 %slices_and_gather.1 = (bf16[2816,256]{1,0:T(8,128)(2,1)S(1)}, bf16[256,512]{1,0:T(8,128)(2,1)S(1)}, bf16[2816,512]{1,0:T(8,128)(2,1)S(1)}, bf16[512,512]{1,0:T(8,128)(2,1)S(1)}, bf16[512,512]{1,0:T(8,128)(2,1)S(1)}) custom-call(bf16[11264,512]{1,0:T(8,128)(2,1)} %x_ref.1, bf16[512,128]{1,0:T(8,128)(2,1)} %ent_ref.1, bf16[32,64]{1,0:T(8,128)(2,1)} %bitcast.2, ...), custom_call_target="tpu_custom_call" | custom-call | tf_op jit(solution)/shard_map/slices_and_gather/pallas_call | solution.py:548
  24.4 5.4 %mix_and_feed.1 = bf16[2816,512]{1,0:T(8,128)(2,1)} custom-call(bf16[2816,256]{1,0:T(8,128)(2,1)S(1)} %get-tuple-element.10.w_ref, bf16[256,512]{1,0:T(8,128)(2,1)S(1)} %get-tuple-element.11.mix_ref, bf16[2816,512]{1,0:T(8,128)(2,1)S(1)} %get-tuple-element.12.x_ref, bf16[512,512]{1,0:T(8,128)(2,1)S(1)} %get-tuple-element.13.upg_ref, ...), custom_call_target="tpu_custom_call" | custom-call | tf_op jit(solution)/shard_map/mix_and_feed/pallas_call | solution.py:599
